TPU v7x, 256 devices: a whole 4x4x8 slice. The times are simulated.
256 devices in a mesh: ep: 64 (over z, y, core), fsdp: 4 (over x).
Axes of the slice: x: 4, y: 4, z: 8, core: 2. Of those that a mesh axis runs over, the one named last changes fastest.
Arguments:
- train_gate: float32 [64, 2048, 1024], P('ep', 'fsdp'), may hold values from -0.1875 to 0.1875
- other_gate: bfloat16 [64, 2048, 1024], P('ep', 'fsdp'), may hold values from -0.0625 to 0.0625
- train_up: float32 [64, 2048, 1024], P('ep', 'fsdp'), may hold values from -0.1875 to 0.1875
- other_up: bfloat16 [64, 2048, 1024], P('ep', 'fsdp'), may hold values from -0.0625 to 0.0625
- router_weight: float32 [2048, 64], P('fsdp', 'ep'), may hold values from -0.125 to 0.125
- router_gain: float32 [2048], P('fsdp'), may hold values from 0.25 to 1.75
Outputs:
- ready_gate: bfloat16 [64, 2048, 1024], P('ep')
- ready_up: bfloat16 [64, 2048, 1024], P('ep')
- scale_gate: float32 [64, 1024], P('ep')
- scale_up: float32 [64, 1024], P('ep')
- serve_router: bfloat16 [2048, 64], replicated
All inputs are finite; a program needn't handle non-finite values.
Results may differ from a plain program's by a relative error of at most 0.001.
Values may be sent and summed in bfloat16 or wider, within the bound.
No kernel may reach another device: no remote copies, remote signals or barrier semaphores. Data moves between devices by JAX's collectives and lax.ppermute only.
A program may use at most 64 MiB of HBM per device.

v0:
```python
import jax
import jax.numpy as jnp
from jax import lax
from jax.sharding import PartitionSpec as P


def copy_for_each(value, axis):
    copies = jnp.broadcast_to(value, (lax.axis_size(axis), *value.shape))
    return lax.all_to_all(copies, axis, split_axis=0, concat_axis=0, tiled=True)


def over_copies(value, axis):
    return copy_for_each(value, axis).sum(axis=0)


def packed_total(arrays, axis):
    flat, at, outs = (jnp.concatenate([a.reshape(-1) for a in arrays]), 0, [])
    so_far = over_copies(flat, axis)
    for a in arrays:
        outs.append(so_far[at : at + a.size].reshape(a.shape))
        at += a.size
    return tuple(outs)


def side_by_side(arrays, axis, dim, along):
    widths = [a.shape[along] for a in arrays]
    both = jnp.concatenate(arrays, axis=along)
    out = lax.all_gather(both, axis, axis=dim, tiled=True)
    return tuple(jnp.split(out, [sum(widths[:k]) for k in range(1, len(widths))], axis=along))


def joined_along(blocks, dim):
    dims = list(blocks.shape[1:])
    dims[dim] *= blocks.shape[0]
    return jnp.moveaxis(blocks, 0, dim).reshape(dims)


def gather_directly(value, axis, dim):
    return joined_along(copy_for_each(value, axis), dim)


def body(train_gate, other_gate, train_up, other_up, router_weight, router_gain):
    latest_gate = train_gate + other_gate.astype(jnp.float32)
    latest_up = train_up + other_up.astype(jnp.float32)
    total_gate, total_up = packed_total(
        (jnp.sum(latest_gate * latest_gate, axis=1), jnp.sum(latest_up * latest_up, axis=1)), "fsdp"
    )
    scale_gate = jnp.sqrt(total_gate)
    scale_up = jnp.sqrt(total_up)
    narrow_gate, narrow_up = (
        (latest_gate / jnp.expand_dims(scale_gate, 1)).astype(jnp.bfloat16),
        (latest_up / jnp.expand_dims(scale_up, 1)).astype(jnp.bfloat16),
    )
    ready_gate, ready_up = side_by_side((narrow_gate, narrow_up), "fsdp", 1, 0)
    part_router = (router_weight * router_gain[:, None]).astype(jnp.bfloat16)
    row_router = lax.all_gather(part_router, "fsdp", axis=0, tiled=True)
    serve_router = gather_directly(row_router, "ep", 1)
    return (ready_gate, ready_up, scale_gate, scale_up, serve_router)


def solution(mesh):
    placed = (
        P("ep", "fsdp", None),
        P("ep", "fsdp", None),
        P("ep", "fsdp", None),
        P("ep", "fsdp", None),
        P("fsdp", "ep"),
        P("fsdp"),
    )
    return jax.shard_map(
        body,
        mesh=mesh,
        in_specs=placed,
        out_specs=(P("ep", None, None), P("ep", None, None), P("ep", None), P("ep", None), P()),
        check_vma=False,
    )
```

profile of v0, /device:TPU:1, one launch (start us, length us, event | category | flops | bytes accessed | tf_op | source)
XLA Modules:
  0.0 124.7 jit_solution(4241068722860294294)
XLA Ops:
  7.2 0.0 copy-start
  7.2 0.0 copy-start.2
  7.2 0.0 all-gather.2.cloned.1.call-start
  7.2 3.6 %multiply_reduce_fusion = (f32[1024]{0:T(1024)S(1)}, f32[1024]{0:T(1024)S(1)}) fusion(f32[1,512,1024]{2,1,0:T(8,128)} %param.8, bf16[1,512,1024]{2,1,0:T(8,128)(2,1)} %param.9, f32[1,512,1024]{2,1,0:T(8,128)} %param.6, bf16[1,512,1024]{2,1,0:T(8,128)(2,1)} %param.7), kind=kLoop, calls=%fused_computation.3 | loop fusion | flops 4192256 | bytes 6299648 | tf_op jit(solution)/shard_map/reduce_sum | solution.py:46
  10.9 8.9 %all_to_all.11 = f32[4,1,2048]{2,1,0:T(1,128)S(1)} all-to-all(f32[4,1,2048]{2,1,0:T(1,128)S(1)} %broadcast_in_dim.11), channel_id=1, replica_groups=mesh['ep'=64,'fsdp'=4] {'fsdp'}, dimensions={0} | all-to-all | bytes 65536 | tf_op jit(solution)/shard_map/all_to_all | solution.py:9
  19.9 0.0 copy-start.5
  19.9 0.0 copy-start.4
  19.9 0.0 copy-done
  19.9 0.0 copy-done.2
  19.9 0.0 copy-start.1
  19.9 0.0 copy-start.3
  20.0 0.4 divide_convert_fusion
  20.3 0.1 copy-done.5
  20.5 0.0 copy-done.4
  20.5 1.0 copy-done.1
  21.5 0.3 copy-done.3
  21.8 0.4 divide_convert_fusion.1
  22.2 1.5 %pad_maximum_fusion = bf16[2,512,1024]{2,1,0:T(8,128)(2,1)} fusion(bf16[1,512,1024]{2,1,0:T(8,128)(2,1)S(1)} %divide_convert_fusion, bf16[1,512,1024]{2,1,0:T(8,128)(2,1)S(1)} %divide_convert_fusion.1), kind=kLoop, calls=%fused_computation | loop fusion | flops 1048576 | bytes 4194304 | tf_op jit(solution)/shard_map/concatenate | solution.py:27
  23.7 0.0 copy-start.6
  23.7 0.0 copy-start.7
  23.7 0.0 all-gather.2.cloned.1.call-update
  23.7 0.7 copy-done.6
  24.4 0.0 copy-done.7
  24.4 8.1 %all_gather.9 = bf16[2048,1]{0,1:T(2,128)(2,1)S(1)} all-gather(bf16[512,1]{0,1:T(2,128)(2,1)S(1)} %multiply_convert_fusion), channel_id=1, replica_groups=mesh['ep'=64,'fsdp'=4] {'fsdp'}, dimensions={0}, use_global_device_ids=true | all-gather | bytes 5120 | tf_op jit(solution)/shard_map/all_gather | solution.py:56
  32.6 0.3 broadcast_bitcast_fusion
  32.8 0.5 broadcast.9
  33.4 2.2 %reduce.4 = bf16[64,2048]{1,0:T(8,128)(2,1)S(1)} reduce(bf16[64,1,2048]{2,1,0:T(2,128)(2,1)S(1)} %broadcast_bitcast_fusion, bf16[]{:T(256)} %broadcast.9), dimensions={1}, to_apply=%broadcast_bitcast_fusion.reduce_sub_computation | reduce | bytes 524290
  35.5 0.2 reshape.38
  35.7 28.9 %all_to_all.12 = bf16[64,2,1024]{2,1,0:T(2,128)(2,1)S(1)} all-to-all(bf16[64,2,1024]{2,1,0:T(2,128)(2,1)S(1)} %reshape.38), channel_id=1, replica_groups=mesh['ep'=64,'fsdp'=4] {'ep'}, dimensions={0} | all-to-all | bytes 524288 | tf_op jit(solution)/shard_map/all_to_all | solution.py:9
  64.6 0.2 reshape.39
  64.9 0.9 copy.19
  65.7 46.1 %all-gather.2.cloned.1.call-done = bf16[2,2048,1024]{2,1,0:T(8,128)(2,1)} async-done(((bf16[2,512,1024]{2,1,0:T(8,128)(2,1)}), bf16[2,2048,1024]{2,1,0:T(8,128)(2,1)}) %all-gather.2.cloned.1.call-update) | async-done | bytes 8388624 | tf_op jit(solution)/shard_map/all_gather | solution.py:28
  111.8 6.0 %fusion = (bf16[1,2048,1024]{2,1,0:T(8,128)(2,1)}, bf16[1,2048,1024]{2,1,0:T(8,128)(2,1)}) fusion(bf16[2,2048,1024]{2,1,0:T(8,128)(2,1)} %all-gather.2.cloned.1.call-done), kind=kLoop, calls=%fused_computation.12 | loop fusion | bytes 16777216 | tf_op jit(solution)/shard_map/split | solution.py:29
  (6 shorter events, 0.1 us)
Async XLA Ops:
  7.2 12.7 %copy-start = (f32[1,512,1024]{2,1,0:T(8,128)S(1)}, f32[1,512,1024]{2,1,0:T(8,128)}, u32[]{:S(2)}) copy-start(f32[1,512,1024]{2,1,0:T(8,128)} %param.8) | copy-start | bytes 6291460
  7.2 12.7 %copy-start.2 = (bf16[1,512,1024]{2,1,0:T(8,128)(2,1)S(1)}, bf16[1,512,1024]{2,1,0:T(8,128)(2,1)}, u32[]{:S(2)}) copy-start(bf16[1,512,1024]{2,1,0:T(8,128)(2,1)} %param.9) | copy-start | bytes 3145732
  7.2 104.7 %all-gather.2.cloned.1.call-start = ((), (), s32[]{:S(2)}) async-start(), calls=%async_computation.2 | async-start | bytes 10485760 | tf_op jit(solution)/shard_map/all_gather | solution.py:28
  19.9 0.6 copy-start.5
  19.9 0.6 copy-start.4
  19.9 1.6 %copy-start.1 = (f32[1,512,1024]{2,1,0:T(8,128)S(1)}, f32[1,512,1024]{2,1,0:T(8,128)}, u32[]{:S(2)}) copy-start(f32[1,512,1024]{2,1,0:T(8,128)} %param.6) | copy-start | bytes 6291460
  19.9 1.8 %copy-start.3 = (bf16[1,512,1024]{2,1,0:T(8,128)(2,1)S(1)}, bf16[1,512,1024]{2,1,0:T(8,128)(2,1)}, u32[]{:S(2)}) copy-start(bf16[1,512,1024]{2,1,0:T(8,128)(2,1)} %param.7) | copy-start | bytes 3145732
  23.7 0.7 copy-start.6
  23.7 0.7 copy-start.7
Sparse Core Ops, SparseCore 0:
  23.8 87.9 all-gather.1
where the time goes:
time: 125 us
  waiting for transfers between devices  46.1 us (37%)
  blocking collectives  46 us (37%)
  between operations  14.2 us (11%)
  local copies, waits for them, and re-layouts  10.2 us (8%)
  other arithmetic  8.13 us (7%)
    all_gather x1, waiting for transfers between devices, side_by_side(): out = lax.all_gather(both, axis, axis=dim, tiled=True)  46.1 us
    all_to_all x2, blocking collectives, copy_for_each(): return lax.all_to_all(copies, axis, split_axis=0, concat_axis=0, tiled=True)  37.9 us
    all_gather x1, blocking collectives, body(): row_router = lax.all_gather(part_router, 'fsdp', axis=0, tiled=True)  8.13 us
    split x1, local copies, waits for them, and re-layouts, side_by_side(): jnp.split(out, [sum(widths[:k]) for k in range(1, len(widths))], axis=along)  6.02 us
    reduce_sum x1, other arithmetic, body(): jnp.sum(latest_up * latest_up, axis=1)  3.63 us
    unnamed x20, local copies, waits for them, and re-layouts  3.34 us
  transfers between devices with their start and end apart: 1, of which 1 were waited for; matrix products, arithmetic and copies ran while one was open for 3% of the time, Pallas kernels for 0%

commit v1 on v0

v1 whole, which is shorter than its diff:
```python
import jax
import jax.numpy as jnp
from jax import lax
from jax.sharding import PartitionSpec as P


def body(train_gate, other_gate, train_up, other_up, router_weight, router_gain):
    n = lax.axis_size("fsdp")
    me = lax.axis_index("fsdp")
    rows, cols = train_gate.shape[1:]

    def shifted(value, by):
        return lax.ppermute(value, "fsdp", [(i, (i + by) % n) for i in range(n)])

    latest = [t[0] + o[0].astype(jnp.float32) for t, o in ((train_gate, other_gate), (train_up, other_up))]
    sums = [jnp.sum(v * v, axis=0) for v in latest]
    small = jnp.concatenate([*sums, router_weight[:, 0] * router_gain])
    small = lax.all_to_all(jnp.broadcast_to(small, (n, small.size)), "fsdp", split_axis=0, concat_axis=0, tiled=True)
    scale = jnp.sqrt(jnp.sum(small[:, : 2 * cols], axis=0)).reshape(2, cols)
    gate, up = [(v / scale[k]).astype(jnp.bfloat16) for k, v in enumerate(latest)]

    gate_left = shifted(gate, 1)
    up_right = shifted(up, n - 1)
    up_left = shifted(up, 1)
    gate_right = shifted(gate, n - 1)
    gate_far = shifted(gate_left, 1)
    up_far = shifted(up_right, n - 1)
    row_router = small[:, 2 * cols :].reshape(-1).astype(jnp.bfloat16)
    e = lax.axis_size("ep")
    copies = jnp.broadcast_to(row_router, (e, row_router.size))
    serve_router = lax.all_to_all(copies, "ep", split_axis=0, concat_axis=0, tiled=True).T

    outs = []
    for own, lefts, rights, far in ((gate, gate_left, gate_right, gate_far), (up, up_left, up_right, up_far)):
        buf = jnp.zeros((n * rows, cols), jnp.bfloat16)
        for piece, by in ((own, 0), (lefts, n - 1), (rights, 1), (far, 2)):
            buf = lax.dynamic_update_slice(buf, piece, ((me + by) % n * rows, 0))
        outs.append(buf[None])
    return (outs[0], outs[1], scale[0:1], scale[1:2], serve_router)


def solution(mesh):
    placed = (
        P("ep", "fsdp", None),
        P("ep", "fsdp", None),
        P("ep", "fsdp", None),
        P("ep", "fsdp", None),
        P("fsdp", "ep"),
        P("fsdp"),
    )
    return jax.shard_map(
        body,
        mesh=mesh,
        in_specs=placed,
        out_specs=(P("ep", None, None), P("ep", None, None), P("ep", None), P("ep", None), P()),
        check_vma=False,
    )
```

time: 125 us -> 89.9 us (0.72)
  the two profiles are of different devices: /device:TPU:1 before, /device:TPU:56 now
where the time goes in v1:
time: 89.9 us; the launch traced here: 89.5 us
  waiting for transfers between devices  32.8 us (36%)
  starting transfers between devices  22.2 us (25%)
  local copies, waits for them, and re-layouts  20.8 us (23%)
  other arithmetic  12.9 us (14%)
    ppermute x6, waiting for transfers between devices, shifted(): return lax.ppermute(value, 'fsdp', [(i, (i + by) % n) for i in range(n)])  24 us
    all_to_all x1, starting transfers between devices, body(): lax.all_to_all(copies, 'ep', split_axis=0, concat_axis=0, tiled=True)  11.4 us
    dynamic_update_slice x6, local copies, waits for them, and re-layouts, body(): buf = lax.dynamic_update_slice(buf, piece, ((me + by) % n * rows, 0))  11.2 us
    ppermute x6, starting transfers between devices, shifted(): return lax.ppermute(value, 'fsdp', [(i, (i + by) % n) for i in range(n)])  6.48 us
    all_to_all x1, waiting for transfers between devices, body(): lax.all_to_all(jnp.broadcast_to(small, (n, small.size)), 'fsdp', split_ax...  5.49 us
    broadcast_in_dim x2, local copies, waits for them, and re-layouts, body(): outs.append(buf[None])  5.09 us
    all_to_all x1, starting transfers between devices, body(): lax.all_to_all(jnp.broadcast_to(small, (n, small.size)), 'fsdp', split_ax...  4.29 us
    reduce_sum x1, other arithmetic, body(): sums = [jnp.sum(v * v, axis=0) for v in latest]  3.63 us
  transfers between devices with their start and end apart: 8, of which 5 were waited for; matrix products, arithmetic and copies ran while one was open for 29% of the time, Pallas kernels for 0%

profile of v1, /device:TPU:56, one launch (start us, length us, event | category | flops | bytes accessed | tf_op | source)
XLA Modules:
  0.0 89.5 jit_solution(3225888825433425934)
XLA Ops:
  0.6 0.7 mul.27
  1.3 0.0 copy-start
  1.3 0.0 copy-start.3
  1.3 3.6 %fusion = (f32[1024]{0:T(1024)S(1)}, f32[1024]{0:T(1024)S(1)}) fusion(f32[1,512,1024]{2,1,0:T(8,128)} %param.8, bf16[1,512,1024]{2,1,0:T(8,128)(2,1)} %param.9, f32[1,512,1024]{2,1,0:T(8,128)} %param.6, bf16[1,512,1024]{2,1,0:T(8,128)(2,1)} %param.7), kind=kLoop, calls=%fused_computation.2 | loop fusion | flops 4192256 | bytes 6299648 | tf_op jit(solution)/shard_map/reduce_sum | solution.py:16
  5.0 0.6 broadcast_in_dim.23
  5.6 4.3 %all-to-all-start = ((f32[4,1,2560]{2,1,0:T(1,128)}), f32[4,1,2560]{2,1,0:T(1,128)S(1)}, u32[]{:S(2)}, u32[]{:S(2)}) async-start(f32[4,1,2560]{2,1,0:T(1,128)} %broadcast_in_dim.23), calls=%async_computation | async-start | bytes 81920 | tf_op jit(solution)/shard_map/all_to_all | solution.py:18
  9.9 5.5 %all-to-all-done = f32[4,1,2560]{2,1,0:T(1,128)S(1)} async-done(((f32[4,1,2560]{2,1,0:T(1,128)}), f32[4,1,2560]{2,1,0:T(1,128)S(1)}, u32[]{:S(2)}, u32[]{:S(2)}) %all-to-all-start) | async-done | bytes 40992 | tf_op jit(solution)/shard_map/all_to_all | solution.py:18
  15.5 0.0 copy-start.6
  15.5 0.0 copy-start.7
  15.5 0.0 copy-done
  15.5 0.0 copy-done.3
  15.5 0.0 copy-start.1
  15.5 0.0 copy-start.4
  15.6 1.4 %fusion.1 = bf16[512,1024]{1,0:T(8,128)(2,1)} fusion(f32[1024]{0:T(1024)S(1)} %get-tuple-element.5, f32[1,512,1024]{2,1,0:T(8,128)S(1)} %copy-done, bf16[1,512,1024]{2,1,0:T(8,128)(2,1)S(1)} %copy-done.3), kind=kLoop, calls=%fused_computation.3 | loop fusion | flops 2097152 | bytes 4198400 | tf_op jit(solution)/shard_map/convert_element_type | solution.py:20
  16.9 0.6 collective-permute-start.3
  17.5 2.7 %collective-permute-start.4 = (bf16[512,1024]{1,0:T(8,128)(2,1)}, bf16[512,1024]{1,0:T(8,128)(2,1)}, u32[]{:S(2)}, u32[]{:S(2)}) collective-permute-start(bf16[512,1024]{1,0:T(8,128)(2,1)} %fusion.1), channel_id=1, source_target_pairs={{0,3},{1,0},{2,1},{3,2},{4,7},{5,4},{6,5},{7,6},{8,11},{9,8},{10,9... | collective-permute-start | bytes 3145736 | tf_op jit(solution)/shard_map/ppermute | solution.py:13
  20.2 0.0 copy-done.1
  20.2 0.0 copy-done.4
  20.2 1.4 %fusion.3 = bf16[512,1024]{1,0:T(8,128)(2,1)} fusion(f32[1024]{0:T(1024)S(1)} %get-tuple-element.6, f32[1,512,1024]{2,1,0:T(8,128)S(1)} %copy-done.1, bf16[1,512,1024]{2,1,0:T(8,128)(2,1)S(1)} %copy-done.4), kind=kLoop, calls=%fused_computation.7 | loop fusion | flops 2097152 | bytes 4198400 | tf_op jit(solution)/shard_map/convert_element_type | solution.py:20
  21.5 0.0 collective-permute-start
  21.5 3.2 %collective-permute-start.1 = (bf16[512,1024]{1,0:T(8,128)(2,1)}, bf16[512,1024]{1,0:T(8,128)(2,1)}, u32[]{:S(2)}, u32[]{:S(2)}) collective-permute-start(bf16[512,1024]{1,0:T(8,128)(2,1)} %fusion.3), channel_id=1, source_target_pairs={{0,3},{1,0},{2,1},{3,2},{4,7},{5,4},{6,5},{7,6},{8,11},{9,8},{10,9... | collective-permute-start | bytes 3145736 | tf_op jit(solution)/shard_map/ppermute | solution.py:13
  24.8 1.1 %broadcast_in_dim.30 = bf16[64,1,2048]{2,1,0:T(2,128)(2,1)} broadcast(bf16[2048]{0:T(1024)(128)(2,1)S(1)} %bitcast.45), dimensions={2} | broadcast | bytes 266240 | tf_op jit(solution)/shard_map/broadcast_in_dim | solution.py:30
  25.8 0.5 broadcast.26
  26.3 3.1 %reduce = bf16[64,2048]{1,0:T(8,128)(2,1)S(1)} reduce(bf16[64,1,2048]{2,1,0:T(2,128)(2,1)} %broadcast_in_dim.30, bf16[]{:T(256)} %broadcast.26), dimensions={1}, to_apply=%broadcast_in_dim.30.reduce_sub_computation | reduce | bytes 524290 | tf_op jit(solution)/shard_map/broadcast_in_dim | solution.py:30
  29.5 0.9 reshape.55
  30.4 11.4 %all-to-all-start.1 = ((bf16[64,2,1024]{2,1,0:T(2,128)(2,1)}), bf16[64,2,1024]{2,1,0:T(2,128)(2,1)S(1)}, u32[]{:S(2)}, u32[]{:S(2)}) async-start(bf16[64,2,1024]{2,1,0:T(2,128)(2,1)} %reshape.55), calls=%async_computation.1 | async-start | bytes 524288 | tf_op jit(solution)/shard_map/all_to_all | solution.py:31
  41.8 2.5 %broadcast_in_dim.22.clone.1 = bf16[1,2048,1024]{2,1,0:T(8,128)(2,1)} broadcast(bf16[]{:T(256)} %constant.49.clone.1), dimensions={} | broadcast | bytes 4194306 | tf_op jit(solution)/shard_map/broadcast_in_dim | solution.py:38
  44.3 0.0 copy-done.6
  44.3 1.3 %fusion.5 = bf16[1,2048,1024]{2,1,0:T(8,128)(2,1)} fusion(bf16[1,2048,1024]{2,1,0:T(8,128)(2,1)} %broadcast_in_dim.22.clone.1, s32[]{:T(128)S(6)} %select_n.44, f32[1024]{0:T(1024)S(1)} %get-tuple-element.5, f32[1,512,1024]{2,1,0:T(8,128)S(1)} %copy-done, bf16[1,512,1024]{2,1,0:T(8,128)(2,1)S(1)} %copy-done.3), kind=kLoop, calls=%fused_computation.13 | loop fusion | flops 2097152 | bytes 4198404 | tf_op jit(solution)/shard_map/dynamic_update_slice | solution.py:37
  45.7 0.0 copy-start.2
  45.7 0.0 copy-start.5
  45.7 2.5 %broadcast_in_dim.22.clone = bf16[1,2048,1024]{2,1,0:T(8,128)(2,1)} broadcast(bf16[]{:T(256)} %constant.49.clone.1), dimensions={} | broadcast | bytes 4194306 | tf_op jit(solution)/shard_map/broadcast_in_dim | solution.py:38
  48.2 0.0 copy-done.7
  48.2 0.0 copy-done.2
  48.2 0.3 copy-done.5
  48.5 1.3 %fusion.4 = bf16[1,2048,1024]{2,1,0:T(8,128)(2,1)} fusion(bf16[1,2048,1024]{2,1,0:T(8,128)(2,1)} %broadcast_in_dim.22.clone, s32[]{:T(128)S(6)} %select_n.44, f32[1024]{0:T(1024)S(1)} %get-tuple-element.6, f32[1,512,1024]{2,1,0:T(8,128)S(1)} %copy-done.2, bf16[1,512,1024]{2,1,0:T(8,128)(2,1)S(1)} %copy-done.5), kind=kLoop, calls=%fused_computation.12 | loop fusion | flops 2097152 | bytes 4198404 | tf_op jit(solution)/shard_map/dynamic_update_slice | solution.py:37
  49.9 3.4 %all-to-all-done.1 = bf16[64,2,1024]{2,1,0:T(2,128)(2,1)S(1)} async-done(((bf16[64,2,1024]{2,1,0:T(2,128)(2,1)}), bf16[64,2,1024]{2,1,0:T(2,128)(2,1)S(1)}, u32[]{:S(2)}, u32[]{:S(2)}) %all-to-all-start.1) | async-done | bytes 262176 | tf_op jit(solution)/shard_map/all_to_all | solution.py:31
  53.2 0.2 reshape.56
  53.5 0.9 copy.16
  54.3 0.0 collective-permute-done.4
  54.3 0.0 collective-permute-start.5
  54.3 10.1 %collective-permute-done = bf16[512,1024]{1,0:T(8,128)(2,1)} collective-permute-done((bf16[512,1024]{1,0:T(8,128)(2,1)}, bf16[512,1024]{1,0:T(8,128)(2,1)}, u32[]{:S(2)}, u32[]{:S(2)}) %collective-permute-start) | collective-permute-done | bytes 1048608 | tf_op jit(solution)/shard_map/ppermute | solution.py:13
  64.4 0.0 collective-permute-start.2
  64.4 2.3 %bitcast_dynamic-update-slice_fusion.5 = bf16[1,2048,1024]{2,1,0:T(8,128)(2,1)} fusion(bf16[1,2048,1024]{2,1,0:T(8,128)(2,1)} %fusion.4, s32[]{:T(128)S(6)} %select_n.46, bf16[512,1024]{1,0:T(8,128)(2,1)} %collective-permute-done), kind=kLoop, calls=%fused_computation.19 | loop fusion | bytes 2097156 | tf_op jit(solution)/shard_map/dynamic_update_slice | solution.py:37
  66.7 0.0 collective-permute-done.3
  66.7 2.3 %bitcast_dynamic-update-slice_fusion.2 = bf16[1,2048,1024]{2,1,0:T(8,128)(2,1)} fusion(bf16[1,2048,1024]{2,1,0:T(8,128)(2,1)} %fusion.5, s32[]{:T(128)S(6)} %select_n.46, bf16[512,1024]{1,0:T(8,128)(2,1)} %collective-permute-done.3), kind=kLoop, calls=%fused_computation.16 | loop fusion | bytes 2097156 | tf_op jit(solution)/shard_map/dynamic_update_slice | solution.py:37
  69.0 2.3 %bitcast_dynamic-update-slice_fusion.1 = bf16[1,2048,1024]{2,1,0:T(8,128)(2,1)} fusion(bf16[1,2048,1024]{2,1,0:T(8,128)(2,1)} %bitcast_dynamic-update-slice_fusion.2, s32[]{:T(128)S(6)} %select_n.48, bf16[512,1024]{1,0:T(8,128)(2,1)} %collective-permute-done.4), kind=kLoop, calls=%fused_computation.15 | loop fusion | bytes 2097156 | tf_op jit(solution)/shard_map/dynamic_update_slice | solution.py:37
  71.2 0.0 collective-permute-done.1
  71.2 2.3 %bitcast_dynamic-update-slice_fusion.4 = bf16[1,2048,1024]{2,1,0:T(8,128)(2,1)} fusion(bf16[1,2048,1024]{2,1,0:T(8,128)(2,1)} %bitcast_dynamic-update-slice_fusion.5, s32[]{:T(128)S(6)} %select_n.48, bf16[512,1024]{1,0:T(8,128)(2,1)} %collective-permute-done.1), kind=kLoop, calls=%fused_computation.18 | loop fusion | bytes 2097156 | tf_op jit(solution)/shard_map/dynamic_update_slice | solution.py:37
  73.5 12.6 %collective-permute-done.5 = bf16[512,1024]{1,0:T(8,128)(2,1)S(1)} collective-permute-done((bf16[512,1024]{1,0:T(8,128)(2,1)}, bf16[512,1024]{1,0:T(8,128)(2,1)S(1)}, u32[]{:S(2)}, u32[]{:S(2)}) %collective-permute-start.5) | collective-permute-done | bytes 1048608 | tf_op jit(solution)/shard_map/ppermute | solution.py:13
  86.1 1.0 %bitcast_dynamic-update-slice_fusion = bf16[1,2048,1024]{2,1,0:T(8,128)(2,1)} fusion(bf16[1,2048,1024]{2,1,0:T(8,128)(2,1)} %bitcast_dynamic-update-slice_fusion.1, s32[]{:T(128)S(6)} %select_n.50, bf16[512,1024]{1,0:T(8,128)(2,1)S(1)} %collective-permute-done.5), kind=kLoop, calls=%fused_computation.14 | loop fusion | bytes 2097156 | tf_op jit(solution)/shard_map/dynamic_update_slice | solution.py:37
  87.2 1.3 %collective-permute-done.2 = bf16[512,1024]{1,0:T(8,128)(2,1)S(1)} collective-permute-done((bf16[512,1024]{1,0:T(8,128)(2,1)}, bf16[512,1024]{1,0:T(8,128)(2,1)S(1)}, u32[]{:S(2)}, u32[]{:S(2)}) %collective-permute-start.2) | collective-permute-done | bytes 1048608 | tf_op jit(solution)/shard_map/ppermute | solution.py:13
  88.4 1.0 %bitcast_dynamic-update-slice_fusion.3 = bf16[1,2048,1024]{2,1,0:T(8,128)(2,1)} fusion(bf16[1,2048,1024]{2,1,0:T(8,128)(2,1)} %bitcast_dynamic-update-slice_fusion.4, s32[]{:T(128)S(6)} %select_n.50, bf16[512,1024]{1,0:T(8,128)(2,1)S(1)} %collective-permute-done.2), kind=kLoop, calls=%fused_computation.17 | loop fusion | bytes 2097156 | tf_op jit(solution)/shard_map/dynamic_update_slice | solution.py:37
  (7 shorter events, 0.1 us)
Async XLA Ops:
  1.3 14.2 %copy-start = (f32[1,512,1024]{2,1,0:T(8,128)S(1)}, f32[1,512,1024]{2,1,0:T(8,128)}, u32[]{:S(2)}) copy-start(f32[1,512,1024]{2,1,0:T(8,128)} %param.8) | copy-start | bytes 6291460
  1.3 14.2 %copy-start.3 = (bf16[1,512,1024]{2,1,0:T(8,128)(2,1)S(1)}, bf16[1,512,1024]{2,1,0:T(8,128)(2,1)}, u32[]{:S(2)}) copy-start(bf16[1,512,1024]{2,1,0:T(8,128)(2,1)} %param.9) | copy-start | bytes 3145732
  5.6 9.8 %all-to-all-start = ((f32[4,1,2560]{2,1,0:T(1,128)}), f32[4,1,2560]{2,1,0:T(1,128)S(1)}, u32[]{:S(2)}, u32[]{:S(2)}) async-start(f32[4,1,2560]{2,1,0:T(1,128)} %broadcast_in_dim.23), calls=%async_computation | async-start | bytes 81920 | tf_op jit(solution)/shard_map/all_to_all | solution.py:18
  15.5 28.9 %copy-start.6 = (f32[1024]{0:T(1024)}, f32[1024]{0:T(1024)S(1)}, u32[]{:S(2)}) copy-start(f32[1024]{0:T(1024)S(1)} %get-tuple-element.5) | copy-start | bytes 12292
  15.5 32.7 %copy-start.7 = (f32[1024]{0:T(1024)}, f32[1024]{0:T(1024)S(1)}, u32[]{:S(2)}) copy-start(f32[1024]{0:T(1024)S(1)} %get-tuple-element.6) | copy-start | bytes 12292
  15.5 4.6 %copy-start.1 = (f32[1,512,1024]{2,1,0:T(8,128)S(1)}, f32[1,512,1024]{2,1,0:T(8,128)}, u32[]{:S(2)}) copy-start(f32[1,512,1024]{2,1,0:T(8,128)} %param.6) | copy-start | bytes 6291460
  15.5 4.6 %copy-start.4 = (bf16[1,512,1024]{2,1,0:T(8,128)(2,1)S(1)}, bf16[1,512,1024]{2,1,0:T(8,128)(2,1)}, u32[]{:S(2)}) copy-start(bf16[1,512,1024]{2,1,0:T(8,128)(2,1)} %param.7) | copy-start | bytes 3145732
  16.9 49.8 %collective-permute-start.3 = (bf16[512,1024]{1,0:T(8,128)(2,1)}, bf16[512,1024]{1,0:T(8,128)(2,1)}, u32[]{:S(2)}, u32[]{:S(2)}) collective-permute-start(bf16[512,1024]{1,0:T(8,128)(2,1)} %fusion.1), channel_id=1, source_target_pairs={{0,1},{1,2},{2,3},{3,0},{4,5},{5,6},{6,7},{7,4},{8,9},{9,10},{10,1... | collective-permute-start | bytes 3145736 | tf_op jit(solution)/shard_map/ppermute | solution.py:13
  17.5 36.8 %collective-permute-start.4 = (bf16[512,1024]{1,0:T(8,128)(2,1)}, bf16[512,1024]{1,0:T(8,128)(2,1)}, u32[]{:S(2)}, u32[]{:S(2)}) collective-permute-start(bf16[512,1024]{1,0:T(8,128)(2,1)} %fusion.1), channel_id=1, source_target_pairs={{0,3},{1,0},{2,1},{3,2},{4,7},{5,4},{6,5},{7,6},{8,11},{9,8},{10,9... | collective-permute-start | bytes 3145736 | tf_op jit(solution)/shard_map/ppermute | solution.py:13
  21.5 42.9 %collective-permute-start = (bf16[512,1024]{1,0:T(8,128)(2,1)}, bf16[512,1024]{1,0:T(8,128)(2,1)}, u32[]{:S(2)}, u32[]{:S(2)}) collective-permute-start(bf16[512,1024]{1,0:T(8,128)(2,1)} %fusion.3), channel_id=1, source_target_pairs={{0,1},{1,2},{2,3},{3,0},{4,5},{5,6},{6,7},{7,4},{8,9},{9,10},{10,1... | collective-permute-start | bytes 3145736 | tf_op jit(solution)/shard_map/ppermute | solution.py:13
  21.5 49.7 %collective-permute-start.1 = (bf16[512,1024]{1,0:T(8,128)(2,1)}, bf16[512,1024]{1,0:T(8,128)(2,1)}, u32[]{:S(2)}, u32[]{:S(2)}) collective-permute-start(bf16[512,1024]{1,0:T(8,128)(2,1)} %fusion.3), channel_id=1, source_target_pairs={{0,3},{1,0},{2,1},{3,2},{4,7},{5,4},{6,5},{7,6},{8,11},{9,8},{10,9... | collective-permute-start | bytes 3145736 | tf_op jit(solution)/shard_map/ppermute | solution.py:13
  30.4 22.9 %all-to-all-start.1 = ((bf16[64,2,1024]{2,1,0:T(2,128)(2,1)}), bf16[64,2,1024]{2,1,0:T(2,128)(2,1)S(1)}, u32[]{:S(2)}, u32[]{:S(2)}) async-start(bf16[64,2,1024]{2,1,0:T(2,128)(2,1)} %reshape.55), calls=%async_computation.1 | async-start | bytes 524288 | tf_op jit(solution)/shard_map/all_to_all | solution.py:31
  45.7 2.6 %copy-start.2 = (f32[1,512,1024]{2,1,0:T(8,128)S(1)}, f32[1,512,1024]{2,1,0:T(8,128)}, u32[]{:S(2)}) copy-start(f32[1,512,1024]{2,1,0:T(8,128)} %param.6) | copy-start | bytes 6291460
  45.7 2.8 %copy-start.5 = (bf16[1,512,1024]{2,1,0:T(8,128)(2,1)S(1)}, bf16[1,512,1024]{2,1,0:T(8,128)(2,1)}, u32[]{:S(2)}) copy-start(bf16[1,512,1024]{2,1,0:T(8,128)(2,1)} %param.7) | copy-start | bytes 3145732
  54.3 31.8 %collective-permute-start.5 = (bf16[512,1024]{1,0:T(8,128)(2,1)}, bf16[512,1024]{1,0:T(8,128)(2,1)S(1)}, u32[]{:S(2)}, u32[]{:S(2)}) collective-permute-start(bf16[512,1024]{1,0:T(8,128)(2,1)} %collective-permute-done.4), channel_id=1, source_target_pairs={{0,3},{1,0},{2,1},{3,2},{4,7},{5,4},{6,5},{7,6},{8,11},{9,8},{10,9... | collective-permute-start | bytes 3145736 | tf_op jit(solution)/shard_map/ppermute | solution.py:13
  64.4 24.0 %collective-permute-start.2 = (bf16[512,1024]{1,0:T(8,128)(2,1)}, bf16[512,1024]{1,0:T(8,128)(2,1)S(1)}, u32[]{:S(2)}, u32[]{:S(2)}) collective-permute-start(bf16[512,1024]{1,0:T(8,128)(2,1)} %collective-permute-done), channel_id=1, source_target_pairs={{0,1},{1,2},{2,3},{3,0},{4,5},{5,6},{6,7},{7,4},{8,9},{9,10},{10,1... | collective-permute-start | bytes 3145736 | tf_op jit(solution)/shard_map/ppermute | solution.py:13

commit v2 on v1

v2 whole, which is shorter than its diff:
```python
import functools

import jax
import jax.numpy as jnp
from jax import lax
from jax.experimental import pallas as pl
from jax.experimental.pallas import tpu as pltpu
from jax.sharding import PartitionSpec as P


RAW = 48
GATE_LAST, UP_LAST, UP_RIGHT = 96, 96, 16
STEP = 64
VMEM = pl.BlockSpec(memory_space=pltpu.VMEM)
ANY = pl.BlockSpec(memory_space=pl.ANY)


def in_vmem(x):
    return pltpu.with_memory_space_constraint(x, pltpu.VMEM)


def in_hbm(x):
    return pltpu.with_memory_space_constraint(x, pltpu.HBM)


def sums_kernel(train_gate, other_gate, train_up, other_up, weight, gain, small, raw, gate, up, train, other, router, sems):
    rows, cols = gate.shape
    steps = rows // STEP
    sources = ((train_gate, other_gate), (train_up, other_up))

    def copies(k, i):
        at = pl.ds(i * STEP, STEP)
        return [
            pltpu.make_async_copy(hbm.at[at], held.at[k, at], sems.at[k, i])
            for hbm, held in zip(sources[k], (train, other))
        ]

    rest = [pltpu.make_async_copy(v, router.at[k], sems.at[2, k]) for k, v in enumerate((weight, gain))]
    for k in range(2):
        for i in range(steps):
            for c in copies(k, i):
                c.start()
        if k == 0:
            for c in rest:
                c.start()
    small[2:] = jnp.zeros((small.shape[0] - 2, cols), jnp.float32)
    for k, latest in enumerate((gate, up)):
        total = jnp.zeros((8, cols), jnp.float32)
        for i in range(steps):
            for c in copies(k, i):
                c.wait()

            def add(j, total):
                at = pl.ds(pl.multiple_of(i * STEP + j * 16, 16), 16)
                v = train[k, at, :] + other[k, at, :].astype(jnp.float32)
                latest[at, :] = v
                return total + (v[:8] * v[:8] + v[8:] * v[8:])

            total = lax.fori_loop(0, STEP // 16, add, total, unroll=True)
            if k == 0 and i == pl.cdiv(RAW, STEP) - 1:
                raw[...] = gate[:RAW]
        small[k : k + 1, :] = jnp.sum(total, axis=0, keepdims=True)
    for c in rest:
        c.wait()
    small[2:3, : weight.shape[1]] = router[0] * router[1]


def sums(*args):
    rows, cols = args[0].shape
    f32 = jnp.float32
    return pl.pallas_call(
        sums_kernel,
        out_shape=(
            pltpu.VMEM((4, cols), f32),
            pltpu.VMEM((RAW, cols), f32),
            pltpu.VMEM((rows, cols), f32),
            pltpu.VMEM((rows, cols), f32),
        ),
        in_specs=[ANY] * 6,
        out_specs=(VMEM,) * 4,
        scratch_shapes=[
            pltpu.VMEM((2, rows, cols), f32),
            pltpu.VMEM((2, rows, cols), jnp.bfloat16),
            pltpu.VMEM((2, *args[4].shape), f32),
            pltpu.SemaphoreType.DMA((3, rows // STEP)),
        ],
        compiler_params=pltpu.CompilerParams(vmem_limit_bytes=20 << 20),
        name="sums",
        cost_estimate=pl.CostEstimate(flops=8 * rows * cols, bytes_accessed=12 * rows * cols, transcendentals=0),
    )(*map(in_hbm, args))


def ready_kernel(row, own, across, left, right, latest, *outs):
    pieces, scale = outs[:-1], outs[-1]
    at = slice(row, row + 1)
    scale[...] = jnp.sqrt((own[at] + across[at]) + (left[at] + right[at]))
    by = scale[...]
    start = 0
    for ref in pieces:

        def divide(j, _, ref=ref, start=start):
            to = pl.ds(pl.multiple_of(j * 16, 16), 16)
            at = pl.ds(pl.multiple_of(start + j * 16, 16), 16)
            ref[to, :] = (latest[at, :] / by).astype(jnp.bfloat16)
            return 0

        lax.fori_loop(0, ref.shape[0] // 16, divide, 0, unroll=2)
        start += ref.shape[0]


def make_ready(row, parts, latest, sizes, near=None):
    rows, cols = latest.shape
    *pieces, scale = pl.pallas_call(
        functools.partial(ready_kernel, row),
        out_shape=(
            *((pltpu.VMEM if size == near else pltpu.HBM)((size, cols), jnp.bfloat16) for size in sizes),
            pltpu.VMEM((1, cols), jnp.float32),
        ),
        in_specs=[VMEM] * 5,
        out_specs=(VMEM,) * (len(sizes) + 1),
        compiler_params=pltpu.CompilerParams(vmem_limit_bytes=8 << 20),
        name="ready",
        cost_estimate=pl.CostEstimate(flops=2 * rows * cols, bytes_accessed=2 * cols, transcendentals=0),
    )(*map(in_vmem, parts), in_vmem(latest))
    return pieces, scale


def place_kernel(rows, count, spots, *refs):
    scratch = 1 + sum(staged for *_, staged in spots)
    outs = refs[-count - scratch : -scratch]
    held, sems = list(refs[-scratch:-1]), refs[-1]
    n = outs[0].shape[0] // rows
    me = lax.axis_index("fsdp")
    ins, copies = [], []
    for k, (out, by, at, staged) in enumerate(spots):
        piece = refs[k]
        if staged:
            stage = held.pop(0)
            ins.append(pltpu.make_async_copy(piece, stage, sems.at[1, k]))
            piece = stage
        else:
            ins.append(None)
        block = lax.rem(me + by, n)
        to = pl.ds(pl.multiple_of(block * rows + at, 16), piece.shape[0])
        copies.append(pltpu.make_async_copy(piece, outs[out].at[to], sems.at[0, k]))
    for c in ins:
        if c is not None:
            c.start()
    for i, c in zip(ins, copies):
        if i is not None:
            i.wait()
        c.start()
    for c in copies:
        c.wait()


def place(rows, n, outs, pieces, staged):
    values = [p[0] for p in pieces]
    used = sorted({p[1] for p in pieces})
    spots = tuple((used.index(p[1]), p[2], p[3], staged) for p in pieces)
    cols = values[0].shape[1]
    given = [outs[k] for k in used if outs[k] is not None]
    done = pl.pallas_call(
        functools.partial(place_kernel, rows, len(used), spots),
        out_shape=tuple(pltpu.HBM((n * rows, cols), jnp.bfloat16) for _ in used),
        in_specs=[ANY if staged else VMEM] * len(values) + [ANY] * len(given),
        out_specs=(ANY,) * len(used),
        scratch_shapes=[
            *(pltpu.VMEM(v.shape, v.dtype) for v in values if staged),
            pltpu.SemaphoreType.DMA((2, len(values))),
        ],
        input_output_aliases={len(values) + k: k for k in range(len(given))},
        compiler_params=pltpu.CompilerParams(vmem_limit_bytes=8 << 20),
        name="place",
        cost_estimate=pl.CostEstimate(
            flops=0, bytes_accessed=sum(2 * v.size * 2 for v in values), transcendentals=0
        ),
    )(*map(in_hbm if staged else in_vmem, values), *map(in_hbm, given))
    outs = list(outs)
    for k, v in zip(used, done):
        outs[k] = v
    return outs


def body(train_gate, other_gate, train_up, other_up, router_weight, router_gain):
    n = lax.axis_size("fsdp")
    rows, _ = train_gate.shape[1:]

    def shifted(value, by):
        return lax.ppermute(value, "fsdp", [(i, (i + by) % n) for i in range(n)])

    small, raw, gate, up = sums(
        train_gate[0],
        other_gate[0],
        train_up[0],
        other_up[0],
        router_weight.reshape(1, -1),
        router_gain.reshape(1, -1),
    )
    parts = (small, shifted(small, 2), shifted(small, 1), shifted(small, n - 1))
    raw_left = shifted(raw, 1)
    raw_right = shifted(raw, n - 1)
    gate_sizes = (RAW, rows - RAW - GATE_LAST, GATE_LAST)
    up_sizes = (rows - UP_LAST - UP_RIGHT, UP_LAST, UP_RIGHT)
    (head, gate0, gate1), scale_gate = make_ready(0, parts, gate, gate_sizes, gate_sizes[1])
    left_gate0 = shifted(gate0, 1)
    right_gate0 = shifted(gate0, n - 1)
    (up0, up1, up2), scale_up = make_ready(1, parts, up, up_sizes)
    left_up, right_up = [], []
    for k, v in enumerate((up0, up1, up2), 1):
        left_up.append(shifted(v, 1))
        right_up.append(shifted(v, n - 1))
    left_gate1 = shifted(gate1, 1)
    right_gate1 = shifted(gate1, n - 1)

    far_gate0 = shifted(left_gate0, 1)
    far_up0 = shifted(right_up[0], n - 1)
    far_up2 = shifted(left_up[2], 1)
    far_up1 = shifted(right_up[1], n - 1)
    far_gate1 = shifted(left_gate1, 1)

    own, across, left, right = [v[2, :rows].astype(jnp.bfloat16) for v in parts]
    turned = jnp.concatenate([own, right, across, left] * 2)
    turned, raw_left, raw_right = lax.optimization_barrier((turned, raw_left, raw_right))
    left_head, right_head = [(v / scale_gate).astype(jnp.bfloat16) for v in (raw_left, raw_right)]
    far_head = shifted(left_head, 1)
    row_router = lax.dynamic_slice(turned, ((n - lax.axis_index("fsdp")) % n * rows,), (n * rows,))
    e = lax.axis_size("ep")
    copies = jnp.broadcast_to(row_router, (e, row_router.size))
    serve_router = lax.all_to_all(copies, "ep", split_axis=0, concat_axis=0, tiled=True).T

    at_gate = (0, RAW, rows - GATE_LAST)
    at_up = (0, rows - UP_LAST - UP_RIGHT, rows - UP_RIGHT)

    def gates(by, *values):
        return [(v, 0, by, at) for v, at in zip(values, at_gate) if v is not None]

    def ups(by, *values):
        return [(v, 1, by, at) for v, at in zip(values, at_up) if v is not None]

    groups = (
        gates(0, head, gate0, gate1) + ups(0, up0, up1, up2),
        gates(n - 1, left_head, left_gate0) + gates(1, right_head, right_gate0),
        ups(n - 1, *left_up) + ups(1, *right_up) + gates(n - 1, None, None, left_gate1) + gates(1, None, None, right_gate1),
        gates(2, far_head, far_gate0) + ups(2, far_up0, None, far_up2),
        gates(2, None, None, far_gate1) + ups(2, None, far_up1),
    )
    outs = [None, None]
    for k, group in enumerate(groups):
        outs = place(rows, n, outs, group, k < 3)
    return (outs[0][None], outs[1][None], scale_gate, scale_up, serve_router)


def solution(mesh):
    placed = (
        P("ep", "fsdp", None),
        P("ep", "fsdp", None),
        P("ep", "fsdp", None),
        P("ep", "fsdp", None),
        P("fsdp", "ep"),
        P("fsdp"),
    )
    return jax.shard_map(
        body,
        mesh=mesh,
        in_specs=placed,
        out_specs=(P("ep", None, None), P("ep", None, None), P("ep", None), P("ep", None), P()),
        check_vma=False,
    )
```

time: 89.9 us -> 125 us (1.39)
  the two profiles are of different devices: /device:TPU:56 before, /device:TPU:1 now
where the time goes in v2:
time: 125 us
  waiting for transfers between devices  52 us (42%)
  starting transfers between devices  45.6 us (36%)
  Pallas kernels  14.9 us (12%)
  local copies, waits for them, and re-layouts  7.17 us (6%)
  other arithmetic  3.87 us (3%)
    ppermute x21, waiting for transfers between devices, shifted(): return lax.ppermute(value, 'fsdp', [(i, (i + by) % n) for i in range(n)])  47.6 us
    all_to_all x1, starting transfers between devices, body(): lax.all_to_all(copies, 'ep', split_axis=0, concat_axis=0, tiled=True)  26.7 us
    ppermute x21, starting transfers between devices, shifted(): return lax.ppermute(value, 'fsdp', [(i, (i + by) % n) for i in range(n)])  18.9 us
    pallas_call x5, Pallas kernels, place(): pl.pallas_call(functools.partial(place_kernel, rows, len(used), spots), o...  9.71 us
    unnamed x26, local copies, waits for them, and re-layouts  6.02 us
    all_to_all x1, waiting for transfers between devices, body(): lax.all_to_all(copies, 'ep', split_axis=0, concat_axis=0, tiled=True)  4.4 us
    pallas_call x1, Pallas kernels, sums(): pl.pallas_call(sums_kernel, out_shape=(pltpu.VMEM((4, cols), f32), pltpu....  3.04 us
  transfers between devices with their start and end apart: 22, of which 8 were waited for; matrix products, arithmetic and copies ran while one was open for 8% of the time, Pallas kernels for 8%

profile of v2, /device:TPU:1, one launch (start us, length us, event | category | flops | bytes accessed | tf_op | source)
XLA Modules:
  0.0 124.6 jit_solution(2153905363642550213)
XLA Ops:
  0.6 3.0 %sums.1 = (f32[4,1024]{1,0:T(4,128)S(1)}, f32[48,1024]{1,0:T(8,128)S(1)}, f32[512,1024]{1,0:T(8,128)S(1)}, f32[512,1024]{1,0:T(8,128)S(1)}) custom-call(f32[512,1024]{1,0:T(8,128)} %bitcast.17, bf16[512,1024]{1,0:T(8,128)(2,1)} %bitcast.19, f32[512,1024]{1,0:T(8,128)} %bitcast.18, bf16[512,1024]{1,0:T(8,128)(2,1)} %bitcast.20, f32[1,512]{1,0:T(1,128)} %bitcast.22, ...), custom_call_target="tpu_custom_call" | custom-call | flops 4194304 | bytes 6291456 | tf_op jit(solution)/shard_map/sums/pallas_call | solution.py:71
  3.7 3.6 %collective-permute-start = (f32[4,1024]{1,0:T(4,128)S(1)}, f32[4,1024]{1,0:T(4,128)S(1)}, u32[]{:S(2)}, u32[]{:S(2)}) collective-permute-start(f32[4,1024]{1,0:T(4,128)S(1)} %get-tuple-element.28.own), channel_id=1, source_target_pairs={{0,2},{1,3},{2,0},{3,1},{4,6},{5,7},{6,4},{7,5},{8,10},{9,11},{10,... | collective-permute-start | bytes 49160 | tf_op jit(solution)/shard_map/ppermute | solution.py:190
  7.3 0.3 collective-permute-start.1
  7.6 2.4 %collective-permute-start.2 = (f32[4,1024]{1,0:T(4,128)S(1)}, f32[4,1024]{1,0:T(4,128)S(1)}, u32[]{:S(2)}, u32[]{:S(2)}) collective-permute-start(f32[4,1024]{1,0:T(4,128)S(1)} %get-tuple-element.28.own), channel_id=1, source_target_pairs={{0,3},{1,0},{2,1},{3,2},{4,7},{5,4},{6,5},{7,6},{8,11},{9,8},{10,9... | collective-permute-start | bytes 49160 | tf_op jit(solution)/shard_map/ppermute | solution.py:190
  10.0 0.0 collective-permute-done.across
  10.0 1.4 %collective-permute-done.1.left = f32[4,1024]{1,0:T(4,128)S(1)} collective-permute-done((f32[4,1024]{1,0:T(4,128)S(1)}, f32[4,1024]{1,0:T(4,128)S(1)}, u32[]{:S(2)}, u32[]{:S(2)}) %collective-permute-start.1) | collective-permute-done | bytes 16416 | tf_op jit(solution)/shard_map/ppermute | solution.py:190
  11.4 0.0 collective-permute-done.2.right
  11.4 1.3 %ready.3 = (bf16[400,1024]{1,0:T(8,128)(2,1)}, bf16[96,1024]{1,0:T(8,128)(2,1)}, bf16[16,1024]{1,0:T(8,128)(2,1)}, f32[1,1024]{1,0:T(1,128)S(1)}) custom-call(f32[4,1024]{1,0:T(4,128)S(1)} %get-tuple-element.28.own, f32[4,1024]{1,0:T(4,128)S(1)} %collective-permute-done.across, f32[4,1024]{1,0:T(4,128)S(1)} %collective-permute-done.1.left, ...), custom_call_target="tpu_custom_call" | custom-call | flops 1048576 | bytes 2048 | tf_op jit(solution)/shard_map/ready/pallas_call | solution.py:113
  12.7 2.4 %collective-permute-start.12 = (bf16[400,1024]{1,0:T(8,128)(2,1)}, bf16[400,1024]{1,0:T(8,128)(2,1)}, u32[]{:S(2)}, u32[]{:S(2)}) collective-permute-start(bf16[400,1024]{1,0:T(8,128)(2,1)} %get-tuple-element.37.refs_3_), channel_id=1, source_target_pairs={{0,3},{1,0},{2,1},{3,2},{4,7},{5,4},{6,5},{7,6},{8,11},{9,8},{10,9... | collective-permute-start | bytes 2457608 | tf_op jit(solution)/shard_map/ppermute | solution.py:190
  15.1 0.9 ready.2
  16.0 0.0 collective-permute-start.10
  16.0 0.0 collective-permute-start.7
  16.0 0.9 collective-permute-start.14
  16.9 1.9 %collective-permute-start.8 = (f32[48,1024]{1,0:T(8,128)S(1)}, f32[48,1024]{1,0:T(8,128)S(1)}, u32[]{:S(2)}, u32[]{:S(2)}) collective-permute-start(f32[48,1024]{1,0:T(8,128)S(1)} %get-tuple-element.33), channel_id=1, source_target_pairs={{0,3},{1,0},{2,1},{3,2},{4,7},{5,4},{6,5},{7,6},{8,11},{9,8},{10,9... | collective-permute-start | bytes 589832 | tf_op jit(solution)/shard_map/ppermute | solution.py:190
  18.8 19.2 %collective-permute-done.14.refs_2_ = bf16[16,1024]{1,0:T(8,128)(2,1)S(1)} collective-permute-done((bf16[16,1024]{1,0:T(8,128)(2,1)}, bf16[16,1024]{1,0:T(8,128)(2,1)S(1)}, u32[]{:S(2)}, u32[]{:S(2)}) %collective-permute-start.14) | collective-permute-done | bytes 32800 | tf_op jit(solution)/shard_map/ppermute | solution.py:190
  38.0 0.0 collective-permute-start.18
  38.0 3.0 %collective-permute-done.18.refs_5_ = bf16[16,1024]{1,0:T(8,128)(2,1)S(1)} collective-permute-done((bf16[16,1024]{1,0:T(8,128)(2,1)}, bf16[16,1024]{1,0:T(8,128)(2,1)S(1)}, u32[]{:S(2)}, u32[]{:S(2)}) %collective-permute-start.18) | collective-permute-done | bytes 32800 | tf_op jit(solution)/shard_map/ppermute | solution.py:190
  41.0 4.0 %collective-permute-done.15.refs_3_ = bf16[16,1024]{1,0:T(8,128)(2,1)S(1)} collective-permute-done((bf16[16,1024]{1,0:T(8,128)(2,1)S(1)}, bf16[16,1024]{1,0:T(8,128)(2,1)S(1)}, u32[]{:S(2)}, u32[]{:S(2)}) %collective-permute-start.15) | collective-permute-done | bytes 32800 | tf_op jit(solution)/shard_map/ppermute | solution.py:190
  45.0 0.0 collective-permute-done.7
  45.0 0.0 collective-permute-start.20
  45.0 0.0 copy-start.2
  45.0 0.7 copy-done.2
  45.7 1.5 %collective-permute-start.3 = (bf16[96,1024]{1,0:T(8,128)(2,1)}, bf16[96,1024]{1,0:T(8,128)(2,1)S(1)}, u32[]{:S(2)}, u32[]{:S(2)}) collective-permute-start(bf16[96,1024]{1,0:T(8,128)(2,1)} %get-tuple-element.30.refs_2_), channel_id=1, source_target_pairs={{0,1},{1,2},{2,3},{3,0},{4,5},{5,6},{6,7},{7,4},{8,9},{9,10},{10,1... | collective-permute-start | bytes 589832 | tf_op jit(solution)/shard_map/ppermute | solution.py:190
  47.1 2.9 %collective-permute-done.5.refs_4_ = bf16[96,1024]{1,0:T(8,128)(2,1)S(1)} collective-permute-done((bf16[96,1024]{1,0:T(8,128)(2,1)}, bf16[96,1024]{1,0:T(8,128)(2,1)S(1)}, u32[]{:S(2)}, u32[]{:S(2)}) %collective-permute-start.5) | collective-permute-done | bytes 196640 | tf_op jit(solution)/shard_map/ppermute | solution.py:190
  50.0 0.2 dynamic-update-slice
  50.3 1.7 %collective-permute-done.3.refs_6_ = bf16[96,1024]{1,0:T(8,128)(2,1)S(1)} collective-permute-done((bf16[96,1024]{1,0:T(8,128)(2,1)}, bf16[96,1024]{1,0:T(8,128)(2,1)S(1)}, u32[]{:S(2)}, u32[]{:S(2)}) %collective-permute-start.3) | collective-permute-done | bytes 196640 | tf_op jit(solution)/shard_map/ppermute | solution.py:190
  52.0 0.0 collective-permute-start.17
  52.0 0.7 copy-done.4
  52.6 1.1 collective-permute-start.11
  53.7 0.0 collective-permute-done.12.refs_3_
  53.7 1.6 %collective-permute-start.13 = (bf16[400,1024]{1,0:T(8,128)(2,1)}, bf16[400,1024]{1,0:T(8,128)(2,1)S(1)}, u32[]{:S(2)}, u32[]{:S(2)}) collective-permute-start(bf16[400,1024]{1,0:T(8,128)(2,1)} %collective-permute-done.12.refs_3_), channel_id=1, source_target_pairs={{0,3},{1,0},{2,1},{3,2},{4,7},{5,4},{6,5},{7,6},{8,11},{9,8},{10,9... | collective-permute-start | bytes 2457608 | tf_op jit(solution)/shard_map/ppermute | solution.py:190
  55.4 15.4 %collective-permute-done.17.refs_1_ = bf16[96,1024]{1,0:T(8,128)(2,1)} collective-permute-done((bf16[96,1024]{1,0:T(8,128)(2,1)}, bf16[96,1024]{1,0:T(8,128)(2,1)}, u32[]{:S(2)}, u32[]{:S(2)}) %collective-permute-start.17) | collective-permute-done | bytes 196640 | tf_op jit(solution)/shard_map/ppermute | solution.py:190
  70.8 0.0 collective-permute-start.19
  70.8 0.2 dynamic-update-slice.1
  71.0 0.2 dynamic-update-slice.2
  71.2 0.2 dynamic-update-slice.3
  71.4 0.2 dynamic-update-slice.4
  71.7 0.2 dynamic-update-slice.5
  71.9 0.2 dynamic-update-slice.6
  72.1 0.2 dynamic-update-slice.7
  72.3 0.1 dynamic_slice.3
  72.3 0.3 broadcast_in_dim.11
  72.6 0.5 broadcast.8
  73.1 2.2 %reduce.8 = bf16[64,2048]{1,0:T(8,128)(2,1)S(1)} reduce(bf16[64,1,2048]{2,1,0:T(2,128)(2,1)S(1)} %broadcast_in_dim.11, bf16[]{:T(256)} %broadcast.8), dimensions={1}, to_apply=%broadcast_in_dim.11.reduce_sub_computation | reduce | bytes 524290 | tf_op jit(solution)/shard_map/broadcast_in_dim | solution.py:229
  75.4 0.9 reshape.30
  76.3 26.7 %all-to-all-start = ((bf16[64,2,1024]{2,1,0:T(2,128)(2,1)}), bf16[64,2,1024]{2,1,0:T(2,128)(2,1)S(1)}, u32[]{:S(2)}, u32[]{:S(2)}) async-start(bf16[64,2,1024]{2,1,0:T(2,128)(2,1)} %reshape.30), calls=%async_computation | async-start | bytes 524288 | tf_op jit(solution)/shard_map/all_to_all | solution.py:230
  103.0 0.2 collective-permute-start.6
  103.1 0.0 collective-permute-done.20.refs_3_
  103.1 1.8 %collective-permute-start.4 = (bf16[96,1024]{1,0:T(8,128)(2,1)}, bf16[96,1024]{1,0:T(8,128)(2,1)S(1)}, u32[]{:S(2)}, u32[]{:S(2)}) collective-permute-start(bf16[96,1024]{1,0:T(8,128)(2,1)} %copy-done.4), channel_id=1, source_target_pairs={{0,1},{1,2},{2,3},{3,0},{4,5},{5,6},{6,7},{7,4},{8,9},{9,10},{10,1... | collective-permute-start | bytes 589832 | tf_op jit(solution)/shard_map/ppermute | solution.py:190
  104.9 1.6 %divide_convert_fusion = (bf16[48,1024]{1,0:T(8,128)(2,1)}, bf16[48,1024]{1,0:T(8,128)(2,1)S(1)}) fusion(f32[48,1024]{1,0:T(8,128)} %copy-done.2, f32[1024]{0:T(1024)S(1)} %bitcast.14, f32[48,1024]{1,0:T(8,128)S(1)} %collective-permute-done.7), kind=kLoop, calls=%fused_computation.1 | loop fusion | flops 196608 | bytes 593920 | tf_op jit(solution)/shard_map/convert_element_type | solution.py:225
  106.5 1.4 %collective-permute-start.9 = (bf16[48,1024]{1,0:T(8,128)(2,1)S(1)}, bf16[48,1024]{1,0:T(8,128)(2,1)S(1)}, u32[]{:S(2)}, u32[]{:S(2)}) collective-permute-start(bf16[48,1024]{1,0:T(8,128)(2,1)S(1)} %get-tuple-element.52.refs_0_), channel_id=1, source_target_pairs={{0,1},{1,2},{2,3},{3,0},{4,5},{5,6},{6,7},{7,4},{8,9},{9,10},{10,1... | collective-permute-start | bytes 294920 | tf_op jit(solution)/shard_map/ppermute | solution.py:190
  107.9 0.6 copy.36
  108.5 2.5 %place.5 = (bf16[2048,1024]{1,0:T(8,128)(2,1)}, bf16[2048,1024]{1,0:T(8,128)(2,1)}) custom-call(bf16[48,1024]{1,0:T(8,128)(2,1)} %get-tuple-element.40.refs_0_, bf16[368,1024]{1,0:T(8,128)(2,1)} %copy-done, bf16[96,1024]{1,0:T(8,128)(2,1)} %get-tuple-element.30.refs_2_, bf16[400,1024]{1,0:T(8,128)(2,1)} %get-tuple-element.37.refs_3_, ...), custom_call_target="tpu_custom_call" | custom-call | bytes 4194304 | tf_op jit(solution)/shard_map/place/pallas_call | solution.py:163
  111.1 0.6 copy.37
  111.7 4.4 %all-to-all-done = bf16[64,2,1024]{2,1,0:T(2,128)(2,1)S(1)} async-done(((bf16[64,2,1024]{2,1,0:T(2,128)(2,1)}), bf16[64,2,1024]{2,1,0:T(2,128)(2,1)S(1)}, u32[]{:S(2)}, u32[]{:S(2)}) %all-to-all-start) | async-done | bytes 262176 | tf_op jit(solution)/shard_map/all_to_all | solution.py:230
  116.1 0.2 reshape.31
  116.3 0.9 copy.20
  117.1 2.4 %place.6.refs_8_ = bf16[2048,1024]{1,0:T(8,128)(2,1)} custom-call(bf16[48,1024]{1,0:T(8,128)(2,1)} %copy-done.1, bf16[368,1024]{1,0:T(8,128)(2,1)} %collective-permute-done.10.refs_1_, bf16[48,1024]{1,0:T(8,128)(2,1)} %get-tuple-element.51.refs_2_, bf16[368,1024]{1,0:T(8,128)(2,1)} %collective-permute-done.20.refs_3_, ...), custom_call_target="tpu_custom_call", output_to_operand_aliasing={{}: (4, {})} | custom-call | bytes 3407872 | tf_op jit(solution)/shard_map/place/pallas_call | solution.py:163
  119.6 2.7 %place.7 = (bf16[2048,1024]{1,0:T(8,128)(2,1)}, bf16[2048,1024]{1,0:T(8,128)(2,1)}) custom-call(bf16[400,1024]{1,0:T(8,128)(2,1)} %collective-permute-done.16.refs_0_, bf16[96,1024]{1,0:T(8,128)(2,1)} %collective-permute-done.17.refs_1_, bf16[16,1024]{1,0:T(8,128)(2,1)} %copy-done.5, ...), custom_call_target="tpu_custom_call", output_to_operand_aliasing={{0}: (8, {}), {1}: (9, {})} | custom-call | bytes 4980736 | tf_op jit(solution)/shard_map/place/pallas_call | solution.py:163
  122.3 0.0 collective-permute-done.9.refs_0_
  122.3 0.0 collective-permute-done.13.refs_2_
  122.3 1.3 %place.8 = (bf16[2048,1024]{1,0:T(8,128)(2,1)}, bf16[2048,1024]{1,0:T(8,128)(2,1)}) custom-call(bf16[48,1024]{1,0:T(8,128)(2,1)S(1)} %collective-permute-done.9.refs_0_, bf16[368,1024]{1,0:T(8,128)(2,1)S(1)} %collective-permute-done.11.refs_1_, bf16[400,1024]{1,0:T(8,128)(2,1)S(1)} %collective-permute-done.13.refs_2_, ...), custom_call_target="tpu_custom_call", output_to_operand_aliasing={{0}: (4, {}), {1}: (5, {})} | custom-call | bytes 3407872 | tf_op jit(solution)/shard_map/place/pallas_call | solution.py:163
  123.6 0.0 collective-permute-done.6.refs_1_
  123.6 0.8 place.9
  (25 shorter events, 0.1 us)
Async XLA Ops:
  3.7 6.3 %collective-permute-start = (f32[4,1024]{1,0:T(4,128)S(1)}, f32[4,1024]{1,0:T(4,128)S(1)}, u32[]{:S(2)}, u32[]{:S(2)}) collective-permute-start(f32[4,1024]{1,0:T(4,128)S(1)} %get-tuple-element.28.own), channel_id=1, source_target_pairs={{0,2},{1,3},{2,0},{3,1},{4,6},{5,7},{6,4},{7,5},{8,10},{9,11},{10,... | collective-permute-start | bytes 49160 | tf_op jit(solution)/shard_map/ppermute | solution.py:190
  7.3 4.1 %collective-permute-start.1 = (f32[4,1024]{1,0:T(4,128)S(1)}, f32[4,1024]{1,0:T(4,128)S(1)}, u32[]{:S(2)}, u32[]{:S(2)}) collective-permute-start(f32[4,1024]{1,0:T(4,128)S(1)} %get-tuple-element.28.own), channel_id=1, source_target_pairs={{0,1},{1,2},{2,3},{3,0},{4,5},{5,6},{6,7},{7,4},{8,9},{9,10},{10,1... | collective-permute-start | bytes 49160 | tf_op jit(solution)/shard_map/ppermute | solution.py:190
  7.6 3.8 %collective-permute-start.2 = (f32[4,1024]{1,0:T(4,128)S(1)}, f32[4,1024]{1,0:T(4,128)S(1)}, u32[]{:S(2)}, u32[]{:S(2)}) collective-permute-start(f32[4,1024]{1,0:T(4,128)S(1)} %get-tuple-element.28.own), channel_id=1, source_target_pairs={{0,3},{1,0},{2,1},{3,2},{4,7},{5,4},{6,5},{7,6},{8,11},{9,8},{10,9... | collective-permute-start | bytes 49160 | tf_op jit(solution)/shard_map/ppermute | solution.py:190
  12.7 41.0 %collective-permute-start.12 = (bf16[400,1024]{1,0:T(8,128)(2,1)}, bf16[400,1024]{1,0:T(8,128)(2,1)}, u32[]{:S(2)}, u32[]{:S(2)}) collective-permute-start(bf16[400,1024]{1,0:T(8,128)(2,1)} %get-tuple-element.37.refs_3_), channel_id=1, source_target_pairs={{0,3},{1,0},{2,1},{3,2},{4,7},{5,4},{6,5},{7,6},{8,11},{9,8},{10,9... | collective-permute-start | bytes 2457608 | tf_op jit(solution)/shard_map/ppermute | solution.py:190
  16.0 92.5 %copy-start = (bf16[368,1024]{1,0:T(8,128)(2,1)}, bf16[368,1024]{1,0:T(8,128)(2,1)S(1)}, u32[]{:S(2)}) copy-start(bf16[368,1024]{1,0:T(8,128)(2,1)S(1)} %get-tuple-element.36.refs_1_) | copy-start | bytes 2260996
  16.0 36.6 %collective-permute-start.10 = (bf16[368,1024]{1,0:T(8,128)(2,1)S(1)}, bf16[368,1024]{1,0:T(8,128)(2,1)}, u32[]{:S(2)}, u32[]{:S(2)}) collective-permute-start(bf16[368,1024]{1,0:T(8,128)(2,1)S(1)} %get-tuple-element.36.refs_1_), channel_id=1, source_target_pairs={{0,1},{1,2},{2,3},{3,0},{4,5},{5,6},{6,7},{7,4},{8,9},{9,10},{10,1... | collective-permute-start | bytes 2261000 | tf_op jit(solution)/shard_map/ppermute | solution.py:190
  16.0 29.0 %collective-permute-start.7 = (f32[48,1024]{1,0:T(8,128)S(1)}, f32[48,1024]{1,0:T(8,128)S(1)}, u32[]{:S(2)}, u32[]{:S(2)}) collective-permute-start(f32[48,1024]{1,0:T(8,128)S(1)} %get-tuple-element.33), channel_id=1, source_target_pairs={{0,1},{1,2},{2,3},{3,0},{4,5},{5,6},{6,7},{7,4},{8,9},{9,10},{10,1... | collective-permute-start | bytes 589832 | tf_op jit(solution)/shard_map/ppermute | solution.py:190
  16.0 22.0 %collective-permute-start.14 = (bf16[16,1024]{1,0:T(8,128)(2,1)}, bf16[16,1024]{1,0:T(8,128)(2,1)S(1)}, u32[]{:S(2)}, u32[]{:S(2)}) collective-permute-start(bf16[16,1024]{1,0:T(8,128)(2,1)} %get-tuple-element.38.refs_5_), channel_id=1, source_target_pairs={{0,1},{1,2},{2,3},{3,0},{4,5},{5,6},{6,7},{7,4},{8,9},{9,10},{10,1... | collective-permute-start | bytes 98312 | tf_op jit(solution)/shard_map/ppermute | solution.py:190
  16.9 28.1 %collective-permute-start.8 = (f32[48,1024]{1,0:T(8,128)S(1)}, f32[48,1024]{1,0:T(8,128)S(1)}, u32[]{:S(2)}, u32[]{:S(2)}) collective-permute-start(f32[48,1024]{1,0:T(8,128)S(1)} %get-tuple-element.33), channel_id=1, source_target_pairs={{0,3},{1,0},{2,1},{3,2},{4,7},{5,4},{6,5},{7,6},{8,11},{9,8},{10,9... | collective-permute-start | bytes 589832 | tf_op jit(solution)/shard_map/ppermute | solution.py:190
  38.0 81.6 %copy-start.5 = (bf16[16,1024]{1,0:T(8,128)(2,1)}, bf16[16,1024]{1,0:T(8,128)(2,1)S(1)}, u32[]{:S(2)}) copy-start(bf16[16,1024]{1,0:T(8,128)(2,1)S(1)} %collective-permute-done.14.refs_2_) | copy-start | bytes 98308
  38.0 3.0 %collective-permute-start.18 = (bf16[16,1024]{1,0:T(8,128)(2,1)}, bf16[16,1024]{1,0:T(8,128)(2,1)S(1)}, u32[]{:S(2)}, u32[]{:S(2)}) collective-permute-start(bf16[16,1024]{1,0:T(8,128)(2,1)} %get-tuple-element.38.refs_5_), channel_id=1, source_target_pairs={{0,3},{1,0},{2,1},{3,2},{4,7},{5,4},{6,5},{7,6},{8,11},{9,8},{10,9... | collective-permute-start | bytes 98312 | tf_op jit(solution)/shard_map/ppermute | solution.py:190
  41.0 78.6 %copy-start.6 = (bf16[16,1024]{1,0:T(8,128)(2,1)}, bf16[16,1024]{1,0:T(8,128)(2,1)S(1)}, u32[]{:S(2)}) copy-start(bf16[16,1024]{1,0:T(8,128)(2,1)S(1)} %collective-permute-done.18.refs_5_) | copy-start | bytes 98308
  41.0 4.0 %collective-permute-start.15 = (bf16[16,1024]{1,0:T(8,128)(2,1)S(1)}, bf16[16,1024]{1,0:T(8,128)(2,1)S(1)}, u32[]{:S(2)}, u32[]{:S(2)}) collective-permute-start(bf16[16,1024]{1,0:T(8,128)(2,1)S(1)} %collective-permute-done.14.refs_2_), channel_id=1, source_target_pairs={{0,1},{1,2},{2,3},{3,0},{4,5},{5,6},{6,7},{7,4},{8,9},{9,10},{10,1... | collective-permute-start | bytes 98312 | tf_op jit(solution)/shard_map/ppermute | solution.py:190
  45.0 5.0 %collective-permute-start.5 = (bf16[96,1024]{1,0:T(8,128)(2,1)}, bf16[96,1024]{1,0:T(8,128)(2,1)S(1)}, u32[]{:S(2)}, u32[]{:S(2)}) collective-permute-start(bf16[96,1024]{1,0:T(8,128)(2,1)} %get-tuple-element.32.refs_4_), channel_id=1, source_target_pairs={{0,3},{1,0},{2,1},{3,2},{4,7},{5,4},{6,5},{7,6},{8,11},{9,8},{10,9... | collective-permute-start | bytes 589832 | tf_op jit(solution)/shard_map/ppermute | solution.py:190
  45.0 58.2 %collective-permute-start.20 = (bf16[368,1024]{1,0:T(8,128)(2,1)S(1)}, bf16[368,1024]{1,0:T(8,128)(2,1)}, u32[]{:S(2)}, u32[]{:S(2)}) collective-permute-start(bf16[368,1024]{1,0:T(8,128)(2,1)S(1)} %get-tuple-element.36.refs_1_), channel_id=1, source_target_pairs={{0,3},{1,0},{2,1},{3,2},{4,7},{5,4},{6,5},{7,6},{8,11},{9,8},{10,9... | collective-permute-start | bytes 2261000 | tf_op jit(solution)/shard_map/ppermute | solution.py:190
  45.0 0.7 copy-start.2
  45.7 6.3 %collective-permute-start.3 = (bf16[96,1024]{1,0:T(8,128)(2,1)}, bf16[96,1024]{1,0:T(8,128)(2,1)S(1)}, u32[]{:S(2)}, u32[]{:S(2)}) collective-permute-start(bf16[96,1024]{1,0:T(8,128)(2,1)} %get-tuple-element.30.refs_2_), channel_id=1, source_target_pairs={{0,1},{1,2},{2,3},{3,0},{4,5},{5,6},{6,7},{7,4},{8,9},{9,10},{10,1... | collective-permute-start | bytes 589832 | tf_op jit(solution)/shard_map/ppermute | solution.py:190
  50.0 2.0 %copy-start.3 = (bf16[96,1024]{1,0:T(8,128)(2,1)}, bf16[96,1024]{1,0:T(8,128)(2,1)S(1)}, u32[]{:S(2)}) copy-start(bf16[96,1024]{1,0:T(8,128)(2,1)S(1)} %collective-permute-done.5.refs_4_) | copy-start | bytes 589828
  50.0 56.6 %collective-permute-start.16 = (bf16[400,1024]{1,0:T(8,128)(2,1)}, bf16[400,1024]{1,0:T(8,128)(2,1)}, u32[]{:S(2)}, u32[]{:S(2)}) collective-permute-start(bf16[400,1024]{1,0:T(8,128)(2,1)} %get-tuple-element.37.refs_3_), channel_id=1, source_target_pairs={{0,1},{1,2},{2,3},{3,0},{4,5},{5,6},{6,7},{7,4},{8,9},{9,10},{10,1... | collective-permute-start | bytes 2457608 | tf_op jit(solution)/shard_map/ppermute | solution.py:190
  52.0 0.7 copy-start.4
  52.0 18.8 %collective-permute-start.17 = (bf16[96,1024]{1,0:T(8,128)(2,1)}, bf16[96,1024]{1,0:T(8,128)(2,1)}, u32[]{:S(2)}, u32[]{:S(2)}) collective-permute-start(bf16[96,1024]{1,0:T(8,128)(2,1)} %get-tuple-element.32.refs_4_), channel_id=1, source_target_pairs={{0,1},{1,2},{2,3},{3,0},{4,5},{5,6},{6,7},{7,4},{8,9},{9,10},{10,1... | collective-permute-start | bytes 589832 | tf_op jit(solution)/shard_map/ppermute | solution.py:190
  52.6 69.7 %collective-permute-start.11 = (bf16[368,1024]{1,0:T(8,128)(2,1)}, bf16[368,1024]{1,0:T(8,128)(2,1)S(1)}, u32[]{:S(2)}, u32[]{:S(2)}) collective-permute-start(bf16[368,1024]{1,0:T(8,128)(2,1)} %collective-permute-done.10.refs_1_), channel_id=1, source_target_pairs={{0,1},{1,2},{2,3},{3,0},{4,5},{5,6},{6,7},{7,4},{8,9},{9,10},{10,1... | collective-permute-start | bytes 2261000 | tf_op jit(solution)/shard_map/ppermute | solution.py:190
  53.7 68.6 %collective-permute-start.13 = (bf16[400,1024]{1,0:T(8,128)(2,1)}, bf16[400,1024]{1,0:T(8,128)(2,1)S(1)}, u32[]{:S(2)}, u32[]{:S(2)}) collective-permute-start(bf16[400,1024]{1,0:T(8,128)(2,1)} %collective-permute-done.12.refs_3_), channel_id=1, source_target_pairs={{0,3},{1,0},{2,1},{3,2},{4,7},{5,4},{6,5},{7,6},{8,11},{9,8},{10,9... | collective-permute-start | bytes 2457608 | tf_op jit(solution)/shard_map/ppermute | solution.py:190
  70.8 32.2 %collective-permute-start.19 = (bf16[96,1024]{1,0:T(8,128)(2,1)}, bf16[96,1024]{1,0:T(8,128)(2,1)}, u32[]{:S(2)}, u32[]{:S(2)}) collective-permute-start(bf16[96,1024]{1,0:T(8,128)(2,1)} %get-tuple-element.30.refs_2_), channel_id=1, source_target_pairs={{0,3},{1,0},{2,1},{3,2},{4,7},{5,4},{6,5},{7,6},{8,11},{9,8},{10,9... | collective-permute-start | bytes 589832 | tf_op jit(solution)/shard_map/ppermute | solution.py:190
  76.3 39.8 %all-to-all-start = ((bf16[64,2,1024]{2,1,0:T(2,128)(2,1)}), bf16[64,2,1024]{2,1,0:T(2,128)(2,1)S(1)}, u32[]{:S(2)}, u32[]{:S(2)}) async-start(bf16[64,2,1024]{2,1,0:T(2,128)(2,1)} %reshape.30), calls=%async_computation | async-start | bytes 524288 | tf_op jit(solution)/shard_map/all_to_all | solution.py:230
  103.0 20.6 %collective-permute-start.6 = (bf16[96,1024]{1,0:T(8,128)(2,1)}, bf16[96,1024]{1,0:T(8,128)(2,1)S(1)}, u32[]{:S(2)}, u32[]{:S(2)}) collective-permute-start(bf16[96,1024]{1,0:T(8,128)(2,1)} %copy-done.3), channel_id=1, source_target_pairs={{0,3},{1,0},{2,1},{3,2},{4,7},{5,4},{6,5},{7,6},{8,11},{9,8},{10,9... | collective-permute-start | bytes 589832 | tf_op jit(solution)/shard_map/ppermute | solution.py:190
  103.1 20.5 %collective-permute-start.4 = (bf16[96,1024]{1,0:T(8,128)(2,1)}, bf16[96,1024]{1,0:T(8,128)(2,1)S(1)}, u32[]{:S(2)}, u32[]{:S(2)}) collective-permute-start(bf16[96,1024]{1,0:T(8,128)(2,1)} %copy-done.4), channel_id=1, source_target_pairs={{0,1},{1,2},{2,3},{3,0},{4,5},{5,6},{6,7},{7,4},{8,9},{9,10},{10,1... | collective-permute-start | bytes 589832 | tf_op jit(solution)/shard_map/ppermute | solution.py:190
  106.5 10.6 %copy-start.1 = (bf16[48,1024]{1,0:T(8,128)(2,1)}, bf16[48,1024]{1,0:T(8,128)(2,1)S(1)}, u32[]{:S(2)}) copy-start(bf16[48,1024]{1,0:T(8,128)(2,1)S(1)} %get-tuple-element.52.refs_0_) | copy-start | bytes 294916
  106.5 15.8 %collective-permute-start.9 = (bf16[48,1024]{1,0:T(8,128)(2,1)S(1)}, bf16[48,1024]{1,0:T(8,128)(2,1)S(1)}, u32[]{:S(2)}, u32[]{:S(2)}) collective-permute-start(bf16[48,1024]{1,0:T(8,128)(2,1)S(1)} %get-tuple-element.52.refs_0_), channel_id=1, source_target_pairs={{0,1},{1,2},{2,3},{3,0},{4,5},{5,6},{6,7},{7,4},{8,9},{9,10},{10,1... | collective-permute-start | bytes 294920 | tf_op jit(solution)/shard_map/ppermute | solution.py:190

commit v3 on v2

v3 whole, which is shorter than its diff:
```python
import functools

import jax
import jax.numpy as jnp
from jax import lax
from jax.experimental import pallas as pl
from jax.experimental.pallas import tpu as pltpu
from jax.sharding import PartitionSpec as P


RAW_NEAR, RAW_WIDE = 64, 48
GATE_LAST, UP_LAST = 96, 96
STEP = 64
LANES = 128
VMEM = pl.BlockSpec(memory_space=pltpu.VMEM)
ANY = pl.BlockSpec(memory_space=pl.ANY)


def in_vmem(x):
    return pltpu.with_memory_space_constraint(x, pltpu.VMEM)


def in_hbm(x):
    return pltpu.with_memory_space_constraint(x, pltpu.HBM)


def sums_kernel(train_gate, other_gate, train_up, other_up, weight, gain, small, raw_near, raw_wide, gate, up, train, other, router, sems):
    rows, cols = up.shape
    steps = rows // STEP
    sources = ((train_gate, other_gate), (train_up, other_up))

    def copies(k, i):
        at = pl.ds(i * STEP, STEP)
        return [
            pltpu.make_async_copy(hbm.at[at], held.at[k, at], sems.at[k, i])
            for hbm, held in zip(sources[k], (train, other))
        ]

    rest = [pltpu.make_async_copy(v, router.at[k], sems.at[2, k]) for k, v in enumerate((weight, gain))]
    for k in range(2):
        for i in range(steps):
            for c in copies(k, i):
                c.start()
        if k == 0:
            for c in rest:
                c.start()
    small[2:] = jnp.zeros((small.shape[0] - 2, cols), jnp.float32)
    for k in range(2):
        total = jnp.zeros((8, cols), jnp.float32)
        for i in range(steps):
            for c in copies(k, i):
                c.wait()

            for row in range(i * STEP, (i + 1) * STEP, 16):
                v = train[k, row : row + 16, :] + other[k, row : row + 16, :].astype(jnp.float32)
                total += v[:8] * v[:8] + v[8:] * v[8:]
                for ref, first in ((up, 0),) if k else ((raw_near, 0), (raw_wide, 0), (gate, RAW_NEAR)):
                    if first <= row < first + ref.shape[0]:
                        ref[row - first : row - first + 16, :] = v
        small[k : k + 1, :] = jnp.sum(total, axis=0, keepdims=True)
    for c in rest:
        c.wait()
    small[2:3, : weight.shape[1]] = router[0] * router[1]


def sums(*args):
    rows, cols = args[0].shape
    f32 = jnp.float32
    return pl.pallas_call(
        sums_kernel,
        out_shape=(
            pltpu.VMEM((4, cols), f32),
            pltpu.VMEM((RAW_NEAR, cols), f32),
            pltpu.VMEM((RAW_WIDE, cols), f32),
            pltpu.VMEM((rows - RAW_NEAR - GATE_LAST, cols), f32),
            pltpu.VMEM((rows, cols), f32),
        ),
        in_specs=[ANY] * 6,
        out_specs=(VMEM,) * 5,
        scratch_shapes=[
            pltpu.VMEM((2, rows, cols), f32),
            pltpu.VMEM((2, rows, cols), jnp.bfloat16),
            pltpu.VMEM((2, *args[4].shape), f32),
            pltpu.SemaphoreType.DMA((3, rows // STEP)),
        ],
        compiler_params=pltpu.CompilerParams(vmem_limit_bytes=20 << 20),
        name="sums",
        cost_estimate=pl.CostEstimate(flops=8 * rows * cols, bytes_accessed=12 * rows * cols, transcendentals=0),
    )(*map(in_hbm, args))


def pair_kernel(own, near, pair):
    half = own.shape[1] // 2
    pair[:2] = own[:2] + near[:2]
    pair[2:3, :half] = own[2:3, :half]
    pair[2:3, half:] = near[2:3, :half]
    pair[3:4] = jnp.zeros((1, 2 * half), jnp.float32)


def add_pair(own, near):
    return pl.pallas_call(
        pair_kernel,
        out_shape=pltpu.VMEM(own.shape, own.dtype),
        in_specs=[VMEM] * 2,
        out_specs=VMEM,
        compiler_params=pltpu.CompilerParams(vmem_limit_bytes=2 << 20),
        name="pair",
        cost_estimate=pl.CostEstimate(flops=2 * own.size, bytes_accessed=own.size, transcendentals=0),
    )(in_vmem(own), in_vmem(near))


def divided(ref, value, scale):
    def divide(j, _):
        at = pl.ds(pl.multiple_of(j * 16, 16), 16)
        ref[at, :] = (value(at) / scale).astype(jnp.bfloat16)
        return 0

    lax.fori_loop(0, ref.shape[0] // 16, divide, 0, unroll=2)


def first_kernel(pair, wide, gate, gate0, scale):
    scale[...] = jnp.sqrt(pair[:1] + wide[:1])
    divided(gate0, lambda at: gate[at, :], scale[...])


def ready_first(pair, wide, gate):
    return pl.pallas_call(
        first_kernel,
        out_shape=(pltpu.VMEM(gate.shape, jnp.bfloat16), pltpu.VMEM((1, gate.shape[1]), jnp.float32)),
        in_specs=[VMEM] * 3,
        out_specs=(VMEM,) * 2,
        compiler_params=pltpu.CompilerParams(vmem_limit_bytes=4 << 20),
        name="ready_first",
        cost_estimate=pl.CostEstimate(flops=2 * gate.size, bytes_accessed=4096, transcendentals=0),
    )(*map(in_vmem, (pair, wide, gate)))


def rest_kernel(pair, wide, up, train_gate, other_gate, up0, up1, gate1, gate_a, gate_b, scale, train, other, sems):
    pieces = ((gate1, train_gate.shape[0] - gate1.shape[0]), (gate_a, 0), (gate_b, gate_a.shape[0]))
    copies, at = [], 0
    for piece, first in pieces:
        for hbm, held in ((train_gate, train), (other_gate, other)):
            size = piece.shape[0]
            copies.append(
                pltpu.make_async_copy(
                    hbm.at[pl.ds(first, size)], held.at[pl.ds(at, size)], sems.at[len(copies)]
                )
            )
        at += piece.shape[0]
    for c in copies:
        c.start()
    scale_gate = jnp.sqrt(pair[:1] + wide[:1])
    scale[...] = jnp.sqrt(pair[1:2] + wide[1:2])
    start = 0
    for piece in (up0, up1):
        divided(piece, lambda at, start=start: up[pl.ds(pl.multiple_of(start + at.start, 16), 16), :], scale[...])
        start += piece.shape[0]
    for c in copies:
        c.wait()
    start = 0
    for piece, _ in pieces:

        def latest(at, start=start):
            at = pl.ds(pl.multiple_of(start + at.start, 16), 16)
            return train[at, :] + other[at, :].astype(jnp.float32)

        divided(piece, latest, scale_gate)
        start += piece.shape[0]


def ready_rest(pair, wide, up, train_gate, other_gate):
    rows, cols = up.shape
    sizes = (rows - UP_LAST, UP_LAST, GATE_LAST, RAW_WIDE, RAW_NEAR - RAW_WIDE)
    return pl.pallas_call(
        rest_kernel,
        out_shape=(
            *(pltpu.HBM((size, cols), jnp.bfloat16) for size in sizes),
            pltpu.VMEM((1, cols), jnp.float32),
        ),
        in_specs=[VMEM] * 3 + [ANY] * 2,
        out_specs=(VMEM,) * (len(sizes) + 1),
        scratch_shapes=[
            pltpu.VMEM((GATE_LAST + RAW_NEAR, cols), jnp.float32),
            pltpu.VMEM((GATE_LAST + RAW_NEAR, cols), jnp.bfloat16),
            pltpu.SemaphoreType.DMA((6,)),
        ],
        compiler_params=pltpu.CompilerParams(vmem_limit_bytes=8 << 20),
        name="ready_rest",
        cost_estimate=pl.CostEstimate(flops=3 * rows * cols, bytes_accessed=3 * rows * cols, transcendentals=0),
    )(*map(in_vmem, (pair, wide, up)), in_hbm(train_gate), in_hbm(other_gate))


def router_kernel(pair, wide, copies, held):
    me = lax.axis_index("fsdp")
    odd, high = lax.rem(me, 2) == 1, me >= 2
    half = pair.shape[1] // 2
    own, near = pair[2:3, :half], pair[2:3, half:]
    across, far = wide[2:3, :half], wide[2:3, half:]
    first = jnp.where(odd, near, own), jnp.where(odd, own, near)
    second = jnp.where(odd, across, far), jnp.where(odd, far, across)
    order = [jnp.where(high, b, a) for a, b in zip(first + second, second + first)]
    for k, part in enumerate(order):
        for c in range(half // LANES):
            row = k * (half // LANES) + c
            held[row : row + 1, :] = part[:, c * LANES : (c + 1) * LANES]
    value = held[...].astype(jnp.bfloat16)

    def copy(k, _):
        copies[k] = value
        return 0

    lax.fori_loop(0, copies.shape[0], copy, 0, unroll=4)


def router_copies(pair, wide, count):
    rows = 2 * pair.shape[1] // LANES
    return pl.pallas_call(
        router_kernel,
        out_shape=jax.ShapeDtypeStruct((count, rows, LANES), jnp.bfloat16),
        in_specs=[VMEM] * 2,
        out_specs=VMEM,
        scratch_shapes=[pltpu.VMEM((rows, LANES), jnp.float32)],
        compiler_params=pltpu.CompilerParams(vmem_limit_bytes=4 << 20),
        name="router",
        cost_estimate=pl.CostEstimate(flops=count, bytes_accessed=2 * count * rows * LANES, transcendentals=0),
    )(pair, wide)


def place_kernel(rows, count, spots, *refs):
    scratch = 1 + sum(staged for *_, staged in spots)
    outs = refs[-count - scratch : -scratch]
    held, sems = list(refs[-scratch:-1]), refs[-1]
    me = lax.axis_index("fsdp")
    blocks = {"own": me, "near": me + 1 - 2 * lax.rem(me, 2), "wide": 3 - me, "far": lax.rem(me + 2, 4)}
    ins, copies = [], []
    for k, (out, owner, at, staged) in enumerate(spots):
        piece = refs[k]
        if staged:
            stage = held.pop(0)
            ins.append(pltpu.make_async_copy(piece, stage, sems.at[1, k]))
            piece = stage
        else:
            ins.append(None)
        to = pl.ds(pl.multiple_of(blocks[owner] * rows + at, 16), piece.shape[0])
        copies.append(pltpu.make_async_copy(piece, outs[out].at[to], sems.at[0, k]))
    for c in ins:
        if c is not None:
            c.start()
    for i, c in zip(ins, copies):
        if i is not None:
            i.wait()
        c.start()
    for c in copies:
        c.wait()


def place(rows, n, outs, pieces, staged):
    values = [p[0] for p in pieces]
    used = sorted({p[1] for p in pieces})
    spots = tuple((used.index(p[1]), p[2], p[3], staged) for p in pieces)
    cols = values[0].shape[1]
    given = [outs[k] for k in used if outs[k] is not None]
    done = pl.pallas_call(
        functools.partial(place_kernel, rows, len(used), spots),
        out_shape=tuple(pltpu.HBM((n * rows, cols), jnp.bfloat16) for _ in used),
        in_specs=[ANY if staged else VMEM] * len(values) + [ANY] * len(given),
        out_specs=(ANY,) * len(used),
        scratch_shapes=[
            *(pltpu.VMEM(v.shape, v.dtype) for v in values if staged),
            pltpu.SemaphoreType.DMA((2, len(values))),
        ],
        input_output_aliases={len(values) + k: k for k in range(len(given))},
        compiler_params=pltpu.CompilerParams(vmem_limit_bytes=8 << 20),
        name="place",
        cost_estimate=pl.CostEstimate(
            flops=0, bytes_accessed=sum(2 * v.size * 2 for v in values), transcendentals=0
        ),
    )(*map(in_hbm if staged else in_vmem, values), *map(in_hbm, given))
    outs = list(outs)
    for k, v in zip(used, done):
        outs[k] = v
    return outs


def body(train_gate, other_gate, train_up, other_up, router_weight, router_gain):
    n = lax.axis_size("fsdp")
    rows, _ = train_gate.shape[1:]

    def exchanged(name, value):
        flip = 3 if "w" in name else 1
        return lax.ppermute(value, "fsdp", [(i, i ^ flip) for i in range(n)])

    small, raw_near, raw_wide, gate, up = sums(
        train_gate[0],
        other_gate[0],
        train_up[0],
        other_up[0],
        router_weight.reshape(1, -1),
        router_gain.reshape(1, -1),
    )
    small_n = exchanged("sum_n", small)
    raw_n = exchanged("early_n", raw_near)
    pair = add_pair(small, small_n)
    pair_w = exchanged("sum_w", pair)
    raw_w = exchanged("early_w", raw_wide)

    at_gate = (0, RAW_WIDE, RAW_NEAR, rows - GATE_LAST)
    at_up = (0, rows - UP_LAST)
    gate0, scale_gate = ready_first(pair, pair_w, gate)
    gate0_n = exchanged("n0", gate0)
    gate0_w = exchanged("w0", gate0)
    up0, up1, gate1, gate_a, gate_b, scale_up = ready_rest(pair, pair_w, up, train_gate[0], other_gate[0])
    up0_n, up1_n, gate1_n = [exchanged(f"n{k}", v) for k, v in enumerate((up0, up1, gate1), 1)]
    gate_b_w, up0_w, up1_w, gate1_w = [exchanged(f"w{k}", v) for k, v in enumerate((gate_b, up0, up1, gate1), 1)]

    late, late_w, raw_n, raw_w, _ = lax.optimization_barrier((pair, pair_w, raw_n, raw_w, up1))
    copies = router_copies(late, late_w, lax.axis_size("ep"))
    columns = lax.all_to_all(copies, "ep", split_axis=0, concat_axis=0, tiled=True)
    serve_router = columns.reshape(columns.shape[0], -1).T

    gate_a_n, gate_b_n, gate_a_w = [
        (v / scale_gate).astype(jnp.bfloat16) for v in (raw_n[:RAW_WIDE], raw_n[RAW_WIDE:], raw_w)
    ]
    far_gate0 = exchanged("far_w0", gate0_n)
    far_up0 = exchanged("far_n0", up0_w)
    far_gate_b = exchanged("far_w1", gate_b_n)
    far_gate_a = exchanged("far_n1", gate_a_w)
    far_up1 = exchanged("far_n2", up1_w)
    far_gate1 = exchanged("far_w2", gate1_n)

    def gates(owner, *values):
        return [(v, 0, owner, at) for v, at in zip(values, at_gate) if v is not None]

    def ups(owner, *values):
        return [(v, 1, owner, at) for v, at in zip(values, at_up) if v is not None]

    groups = (
        gates("own", gate_a, gate_b, gate0, gate1) + ups("own", up0, up1),
        gates("near", gate_a_n, gate_b_n, gate0_n) + gates("wide", gate_a_w, gate_b_w, gate0_w),
        gates("near", None, None, None, gate1_n)
        + gates("wide", None, None, None, gate1_w)
        + ups("near", up0_n, up1_n)
        + ups("wide", up0_w, up1_w),
        gates("far", far_gate_a, far_gate_b, far_gate0) + ups("far", far_up0),
        gates("far", None, None, None, far_gate1) + ups("far", None, far_up1),
    )
    outs = [None, None]
    for k, group in enumerate(groups):
        outs = place(rows, n, outs, group, k < 3)
    return (outs[0][None], outs[1][None], scale_gate, scale_up, serve_router)


def solution(mesh):
    placed = (
        P("ep", "fsdp", None),
        P("ep", "fsdp", None),
        P("ep", "fsdp", None),
        P("ep", "fsdp", None),
        P("fsdp", "ep"),
        P("fsdp"),
    )
    return jax.shard_map(
        body,
        mesh=mesh,
        in_specs=placed,
        out_specs=(P("ep", None, None), P("ep", None, None), P("ep", None), P("ep", None), P()),
        check_vma=False,
    )
```

time: 125 us -> 124 us (level)
  the two profiles are of different devices: /device:TPU:1 before, /device:TPU:128 now
where the time goes in v3:
time: 124 us; the launch traced here: 123 us
  waiting for transfers between devices  64.1 us (52%)
  starting transfers between devices  38.9 us (31%)
  Pallas kernels  16.2 us (13%)
  local copies, waits for them, and re-layouts  2.66 us (2%)
    ppermute x19, waiting for transfers between devices, exchanged(): return lax.ppermute(value, 'fsdp', [(i, i ^ flip) for i in range(n)])  64.1 us
    ppermute x19, starting transfers between devices, exchanged(): return lax.ppermute(value, 'fsdp', [(i, i ^ flip) for i in range(n)])  28.5 us
    all_to_all x1, starting transfers between devices, body(): lax.all_to_all(copies, 'ep', split_axis=0, concat_axis=0, tiled=True)  10.5 us
    pallas_call x5, Pallas kernels, place(): pl.pallas_call(functools.partial(place_kernel, rows, len(used), spots), o...  9.82 us
    pallas_call x1, Pallas kernels, sums(): pl.pallas_call(sums_kernel, out_shape=(pltpu.VMEM((4, cols), f32), pltpu....  3.05 us
    unnamed x15, local copies, waits for them, and re-layouts  2.66 us
  transfers between devices with their start and end apart: 20, of which 8 were waited for; matrix products, arithmetic and copies ran while one was open for 2% of the time, Pallas kernels for 8%

profile of v3, /device:TPU:128, one launch (start us, length us, event | category | flops | bytes accessed | tf_op | source)
XLA Modules:
  0.0 123.4 jit_solution(1025984830879290423)
XLA Ops:
  0.6 3.0 %sums.1 = (f32[4,1024]{1,0:T(4,128)S(1)}, f32[64,1024]{1,0:T(8,128)S(1)}, f32[48,1024]{1,0:T(8,128)S(1)}, f32[352,1024]{1,0:T(8,128)S(1)}, f32[512,1024]{1,0:T(8,128)S(1)}) custom-call(f32[512,1024]{1,0:T(8,128)} %bitcast.20, bf16[512,1024]{1,0:T(8,128)(2,1)} %bitcast.22, f32[512,1024]{1,0:T(8,128)} %bitcast.24, bf16[512,1024]{1,0:T(8,128)(2,1)} %bitcast.26, ...), custom_call_target="tpu_custom_call" | custom-call | flops 4194304 | bytes 6291456 | tf_op jit(solution)/shard_map/sums/pallas_call | solution.py:69
  3.7 1.6 %collective-permute-start = (f32[4,1024]{1,0:T(4,128)S(1)}, f32[4,1024]{1,0:T(4,128)S(1)}, u32[]{:S(2)}, u32[]{:S(2)}) collective-permute-start(f32[4,1024]{1,0:T(4,128)S(1)} %get-tuple-element.30.own), channel_id=1, source_target_pairs={{0,1},{1,0},{2,3},{3,2},{4,5},{5,4},{6,7},{7,6},{8,9},{9,8},{10,11... | collective-permute-start | bytes 49160 | tf_op jit(solution)/shard_map/ppermute | solution.py:291
  5.3 2.2 %collective-permute-done.near = f32[4,1024]{1,0:T(4,128)S(1)} collective-permute-done((f32[4,1024]{1,0:T(4,128)S(1)}, f32[4,1024]{1,0:T(4,128)S(1)}, u32[]{:S(2)}, u32[]{:S(2)}) %collective-permute-start) | collective-permute-done | bytes 16416 | tf_op jit(solution)/shard_map/ppermute | solution.py:291
  7.5 2.8 %collective-permute-start.1 = (f32[4,1024]{1,0:T(4,128)S(1)}, f32[4,1024]{1,0:T(4,128)S(1)}, u32[]{:S(2)}, u32[]{:S(2)}) collective-permute-start(f32[4,1024]{1,0:T(4,128)S(1)} %pair.1), channel_id=1, source_target_pairs={{0,3},{1,2},{2,1},{3,0},{4,7},{5,6},{6,5},{7,4},{8,11},{9,10},{10,... | collective-permute-start | bytes 49160 | tf_op jit(solution)/shard_map/ppermute | solution.py:291
  10.3 2.2 %collective-permute-done.1.wide = f32[4,1024]{1,0:T(4,128)S(1)} collective-permute-done((f32[4,1024]{1,0:T(4,128)S(1)}, f32[4,1024]{1,0:T(4,128)S(1)}, u32[]{:S(2)}, u32[]{:S(2)}) %collective-permute-start.1) | collective-permute-done | bytes 16416 | tf_op jit(solution)/shard_map/ppermute | solution.py:291
  12.5 2.4 %ready_rest.1 = (bf16[416,1024]{1,0:T(8,128)(2,1)}, bf16[96,1024]{1,0:T(8,128)(2,1)}, bf16[96,1024]{1,0:T(8,128)(2,1)}, bf16[48,1024]{1,0:T(8,128)(2,1)}, bf16[1...) custom-call(f32[4,1024]{1,0:T(4,128)S(1)} %pair.1, f32[4,1024]{1,0:T(4,128)S(1)} %collective-permute-done.1.wide, ...), custom_call_target="tpu_custom_call" | custom-call | flops 1572864 | bytes 1572864 | tf_op jit(solution)/shard_map/ready_rest/pallas_call | solution.py:174
  14.8 2.8 %collective-permute-start.12 = (bf16[416,1024]{1,0:T(8,128)(2,1)}, bf16[416,1024]{1,0:T(8,128)(2,1)}, u32[]{:S(2)}, u32[]{:S(2)}) collective-permute-start(bf16[416,1024]{1,0:T(8,128)(2,1)} %get-tuple-element.41.refs_4_), channel_id=1, source_target_pairs={{0,3},{1,2},{2,1},{3,0},{4,7},{5,6},{6,5},{7,4},{8,11},{9,10},{10,... | collective-permute-start | bytes 2555912 | tf_op jit(solution)/shard_map/ppermute | solution.py:291
  17.7 0.2 ready_first.1
  17.9 0.0 copy-start
  17.9 0.1 collective-permute-start.10
  18.0 0.6 collective-permute-start.7
  18.5 2.8 %collective-permute-start.4 = (bf16[96,1024]{1,0:T(8,128)(2,1)}, bf16[96,1024]{1,0:T(8,128)(2,1)S(1)}, u32[]{:S(2)}, u32[]{:S(2)}) collective-permute-start(bf16[96,1024]{1,0:T(8,128)(2,1)} %get-tuple-element.33.refs_5_), channel_id=1, source_target_pairs={{0,3},{1,2},{2,1},{3,0},{4,7},{5,6},{6,5},{7,4},{8,11},{9,10},{10,... | collective-permute-start | bytes 589832 | tf_op jit(solution)/shard_map/ppermute | solution.py:291
  21.3 0.5 collective-permute-start.17
  21.8 22.2 %collective-permute-done.17.refs_4_ = bf16[16,1024]{1,0:T(8,128)(2,1)} collective-permute-done((bf16[16,1024]{1,0:T(8,128)(2,1)}, bf16[16,1024]{1,0:T(8,128)(2,1)}, u32[]{:S(2)}, u32[]{:S(2)}) %collective-permute-start.17) | collective-permute-done | bytes 32800 | tf_op jit(solution)/shard_map/ppermute | solution.py:291
  44.0 0.0 collective-permute-start.16
  44.0 0.0 collective-permute-done.7
  44.0 2.8 %collective-permute-start.18 = (bf16[352,1024]{1,0:T(8,128)(2,1)S(1)}, bf16[352,1024]{1,0:T(8,128)(2,1)}, u32[]{:S(2)}, u32[]{:S(2)}) collective-permute-start(bf16[352,1024]{1,0:T(8,128)(2,1)S(1)} %get-tuple-element.40.refs_2_), channel_id=1, source_target_pairs={{0,3},{1,2},{2,1},{3,0},{4,7},{5,6},{6,5},{7,4},{8,11},{9,10},{10,... | collective-permute-start | bytes 2162696 | tf_op jit(solution)/shard_map/ppermute | solution.py:291
  46.7 0.0 collective-permute-done.4.refs_5_
  46.7 0.0 copy-start.2
  46.7 1.4 %collective-permute-start.6 = (f32[64,1024]{1,0:T(8,128)S(1)}, f32[64,1024]{1,0:T(8,128)S(1)}, u32[]{:S(2)}, u32[]{:S(2)}) collective-permute-start(f32[64,1024]{1,0:T(8,128)S(1)} %get-tuple-element.34), channel_id=1, source_target_pairs={{0,1},{1,0},{2,3},{3,2},{4,5},{5,4},{6,7},{7,6},{8,9},{9,8},{10,11... | collective-permute-start | bytes 786440 | tf_op jit(solution)/shard_map/ppermute | solution.py:291
  48.2 3.8 %collective-permute-done.16.refs_3_ = bf16[96,1024]{1,0:T(8,128)(2,1)S(1)} collective-permute-done((bf16[96,1024]{1,0:T(8,128)(2,1)}, bf16[96,1024]{1,0:T(8,128)(2,1)S(1)}, u32[]{:S(2)}, u32[]{:S(2)}) %collective-permute-start.16) | collective-permute-done | bytes 196640 | tf_op jit(solution)/shard_map/ppermute | solution.py:291
  51.9 0.0 copy-start.3
  51.9 0.0 collective-permute-start.15
  52.0 0.0 copy-done.2
  52.0 0.7 copy-done.3
  52.6 0.0 collective-permute-done.12.refs_4_
  52.6 1.4 %collective-permute-start.13 = (bf16[416,1024]{1,0:T(8,128)(2,1)}, bf16[416,1024]{1,0:T(8,128)(2,1)S(1)}, u32[]{:S(2)}, u32[]{:S(2)}) collective-permute-start(bf16[416,1024]{1,0:T(8,128)(2,1)} %collective-permute-done.12.refs_4_), channel_id=1, source_target_pairs={{0,1},{1,0},{2,3},{3,2},{4,5},{5,4},{6,7},{7,6},{8,9},{9,8},{10,11... | collective-permute-start | bytes 2555912 | tf_op jit(solution)/shard_map/ppermute | solution.py:291
  54.1 3.5 %collective-permute-done.6 = f32[64,1024]{1,0:T(8,128)S(1)} collective-permute-done((f32[64,1024]{1,0:T(8,128)S(1)}, f32[64,1024]{1,0:T(8,128)S(1)}, u32[]{:S(2)}, u32[]{:S(2)}) %collective-permute-start.6) | collective-permute-done | bytes 262176 | tf_op jit(solution)/shard_map/ppermute | solution.py:291
  57.6 0.0 collective-permute-start.2
  57.6 0.0 collective-permute-done.10.refs_2_
  57.6 2.8 %collective-permute-start.11 = (bf16[352,1024]{1,0:T(8,128)(2,1)}, bf16[352,1024]{1,0:T(8,128)(2,1)S(1)}, u32[]{:S(2)}, u32[]{:S(2)}) collective-permute-start(bf16[352,1024]{1,0:T(8,128)(2,1)} %collective-permute-done.10.refs_2_), channel_id=1, source_target_pairs={{0,3},{1,2},{2,1},{3,0},{4,7},{5,6},{6,5},{7,4},{8,11},{9,10},{10,... | collective-permute-start | bytes 2162696 | tf_op jit(solution)/shard_map/ppermute | solution.py:291
  60.3 0.8 router.1
  61.1 10.5 %all-to-all-start = ((bf16[64,16,128]{2,1,0:T(8,128)(2,1)}), bf16[64,16,128]{2,1,0:T(8,128)(2,1)S(1)}, u32[]{:S(2)}, u32[]{:S(2)}) async-start(bf16[64,16,128]{2,1,0:T(8,128)(2,1)} %router.1), calls=%async_computation | async-start | bytes 524288 | tf_op jit(solution)/shard_map/all_to_all | solution.py:318
  71.6 22.6 %collective-permute-done.2.refs_0_ = bf16[96,1024]{1,0:T(8,128)(2,1)} collective-permute-done((bf16[96,1024]{1,0:T(8,128)(2,1)}, bf16[96,1024]{1,0:T(8,128)(2,1)}, u32[]{:S(2)}, u32[]{:S(2)}) %collective-permute-start.2) | collective-permute-done | bytes 196640 | tf_op jit(solution)/shard_map/ppermute | solution.py:291
  94.2 2.6 %collective-permute-start.14 = (bf16[96,1024]{1,0:T(8,128)(2,1)}, bf16[96,1024]{1,0:T(8,128)(2,1)S(1)}, u32[]{:S(2)}, u32[]{:S(2)}) collective-permute-start(bf16[96,1024]{1,0:T(8,128)(2,1)} %get-tuple-element.32.refs_3_), channel_id=1, source_target_pairs={{0,3},{1,2},{2,1},{3,0},{4,7},{5,6},{6,5},{7,4},{8,11},{9,10},{10,... | collective-permute-start | bytes 589832 | tf_op jit(solution)/shard_map/ppermute | solution.py:291
  96.8 0.0 copy-start.5
  96.8 4.8 %collective-permute-done.14.refs_1_ = bf16[96,1024]{1,0:T(8,128)(2,1)S(1)} collective-permute-done((bf16[96,1024]{1,0:T(8,128)(2,1)}, bf16[96,1024]{1,0:T(8,128)(2,1)S(1)}, u32[]{:S(2)}, u32[]{:S(2)}) %collective-permute-start.14) | collective-permute-done | bytes 196640 | tf_op jit(solution)/shard_map/ppermute | solution.py:291
  101.6 0.0 copy-start.4
  101.6 2.6 %collective-permute-start.9 = (bf16[16,1024]{1,0:T(8,128)(2,1)S(1)}, bf16[16,1024]{1,0:T(8,128)(2,1)S(1)}, u32[]{:S(2)}, u32[]{:S(2)}) collective-permute-start(bf16[16,1024]{1,0:T(8,128)(2,1)S(1)} %divide_convert_fusion.2.refs_1_), channel_id=1, source_target_pairs={{0,3},{1,2},{2,1},{3,0},{4,7},{5,6},{6,5},{7,4},{8,11},{9,10},{10,... | collective-permute-start | bytes 98312 | tf_op jit(solution)/shard_map/ppermute | solution.py:291
  104.2 0.0 copy-done.4
  104.2 2.8 %collective-permute-done.9.refs_1_ = bf16[16,1024]{1,0:T(8,128)(2,1)S(1)} collective-permute-done((bf16[16,1024]{1,0:T(8,128)(2,1)S(1)}, bf16[16,1024]{1,0:T(8,128)(2,1)S(1)}, u32[]{:S(2)}, u32[]{:S(2)}) %collective-permute-start.9) | collective-permute-done | bytes 32800 | tf_op jit(solution)/shard_map/ppermute | solution.py:291
  107.0 0.0 collective-permute-start.5
  107.0 0.0 collective-permute-done.18.refs_5_
  107.0 2.4 %collective-permute-start.3 = (bf16[96,1024]{1,0:T(8,128)(2,1)}, bf16[96,1024]{1,0:T(8,128)(2,1)S(1)}, u32[]{:S(2)}, u32[]{:S(2)}) collective-permute-start(bf16[96,1024]{1,0:T(8,128)(2,1)} %collective-permute-done.2.refs_0_), channel_id=1, source_target_pairs={{0,3},{1,2},{2,1},{3,0},{4,7},{5,6},{6,5},{7,4},{8,11},{9,10},{10,... | collective-permute-start | bytes 589832 | tf_op jit(solution)/shard_map/ppermute | solution.py:291
  109.4 0.7 divide_convert_fusion
  110.1 0.0 collective-permute-done.15.refs_2_
  110.1 1.4 %collective-permute-start.8 = (bf16[48,1024]{1,0:T(8,128)(2,1)S(1)}, bf16[48,1024]{1,0:T(8,128)(2,1)S(1)}, u32[]{:S(2)}, u32[]{:S(2)}) collective-permute-start(bf16[48,1024]{1,0:T(8,128)(2,1)S(1)} %get-tuple-element.56.refs_3_), channel_id=1, source_target_pairs={{0,1},{1,0},{2,3},{3,2},{4,5},{5,4},{6,7},{7,6},{8,9},{9,8},{10,11... | collective-permute-start | bytes 294920 | tf_op jit(solution)/shard_map/ppermute | solution.py:291
  111.5 0.6 copy.28
  112.1 0.0 copy-done
  112.1 2.6 %place.5 = (bf16[2048,1024]{1,0:T(8,128)(2,1)}, bf16[2048,1024]{1,0:T(8,128)(2,1)}) custom-call(bf16[48,1024]{1,0:T(8,128)(2,1)} %get-tuple-element.43.refs_0_, bf16[16,1024]{1,0:T(8,128)(2,1)} %get-tuple-element.42.refs_1_, bf16[352,1024]{1,0:T(8,128)(2,1)} %copy-done, bf16[96,1024]{1,0:T(8,128)(2,1)} %get-tuple-element.32.refs_3_, ...), custom_call_target="tpu_custom_call" | custom-call | bytes 4194304 | tf_op jit(solution)/shard_map/place/pallas_call | solution.py:263
  114.7 0.6 copy.29
  115.3 0.0 copy-done.5
  115.3 0.0 copy-done.1
  115.3 2.4 %place.6.refs_6_ = bf16[2048,1024]{1,0:T(8,128)(2,1)} custom-call(bf16[48,1024]{1,0:T(8,128)(2,1)} %get-tuple-element.55.refs_0_, bf16[16,1024]{1,0:T(8,128)(2,1)} %copy-done.5, bf16[352,1024]{1,0:T(8,128)(2,1)} %collective-permute-done.10.refs_2_, bf16[48,1024]{1,0:T(8,128)(2,1)} %copy-done.1, ...), custom_call_target="tpu_custom_call", output_to_operand_aliasing={{}: (6, {})} | custom-call | bytes 3407872 | tf_op jit(solution)/shard_map/place/pallas_call | solution.py:263
  117.7 0.0 all-to-all-done
  117.7 0.8 copy.20
  118.5 2.8 %place.7 = (bf16[2048,1024]{1,0:T(8,128)(2,1)}, bf16[2048,1024]{1,0:T(8,128)(2,1)}) custom-call(bf16[96,1024]{1,0:T(8,128)(2,1)} %collective-permute-done.2.refs_0_, bf16[96,1024]{1,0:T(8,128)(2,1)} %copy-done.4, bf16[416,1024]{1,0:T(8,128)(2,1)} %collective-permute-done.15.refs_2_, ...), custom_call_target="tpu_custom_call", output_to_operand_aliasing={{0}: (6, {}), {1}: (7, {})} | custom-call | bytes 4980736 | tf_op jit(solution)/shard_map/place/pallas_call | solution.py:263
  121.3 0.0 collective-permute-done.8.refs_0_
  121.3 0.0 collective-permute-done.11.refs_2_
  121.3 0.0 collective-permute-done.13.refs_3_
  121.3 1.3 %place.8 = (bf16[2048,1024]{1,0:T(8,128)(2,1)}, bf16[2048,1024]{1,0:T(8,128)(2,1)}) custom-call(bf16[48,1024]{1,0:T(8,128)(2,1)S(1)} %collective-permute-done.8.refs_0_, bf16[16,1024]{1,0:T(8,128)(2,1)S(1)} %collective-permute-done.9.refs_1_, bf16[352,1024]{1,0:T(8,128)(2,1)S(1)} %collective-permute-done.11.refs_2_, ...), custom_call_target="tpu_custom_call", output_to_operand_aliasing={{0}: (4, {}), {1}: (5, {})} | custom-call | bytes 3407872 | tf_op jit(solution)/shard_map/place/pallas_call | solution.py:263
  122.6 0.0 collective-permute-done.5.refs_1_
  122.6 0.0 collective-permute-done.3.refs_0_
  122.6 0.8 place.9
  (3 shorter events, 0.0 us)
Async XLA Ops:
  3.7 3.8 %collective-permute-start = (f32[4,1024]{1,0:T(4,128)S(1)}, f32[4,1024]{1,0:T(4,128)S(1)}, u32[]{:S(2)}, u32[]{:S(2)}) collective-permute-start(f32[4,1024]{1,0:T(4,128)S(1)} %get-tuple-element.30.own), channel_id=1, source_target_pairs={{0,1},{1,0},{2,3},{3,2},{4,5},{5,4},{6,7},{7,6},{8,9},{9,8},{10,11... | collective-permute-start | bytes 49160 | tf_op jit(solution)/shard_map/ppermute | solution.py:291
  7.5 4.9 %collective-permute-start.1 = (f32[4,1024]{1,0:T(4,128)S(1)}, f32[4,1024]{1,0:T(4,128)S(1)}, u32[]{:S(2)}, u32[]{:S(2)}) collective-permute-start(f32[4,1024]{1,0:T(4,128)S(1)} %pair.1), channel_id=1, source_target_pairs={{0,3},{1,2},{2,1},{3,0},{4,7},{5,6},{6,5},{7,4},{8,11},{9,10},{10,... | collective-permute-start | bytes 49160 | tf_op jit(solution)/shard_map/ppermute | solution.py:291
  14.8 37.8 %collective-permute-start.12 = (bf16[416,1024]{1,0:T(8,128)(2,1)}, bf16[416,1024]{1,0:T(8,128)(2,1)}, u32[]{:S(2)}, u32[]{:S(2)}) collective-permute-start(bf16[416,1024]{1,0:T(8,128)(2,1)} %get-tuple-element.41.refs_4_), channel_id=1, source_target_pairs={{0,3},{1,2},{2,1},{3,0},{4,7},{5,6},{6,5},{7,4},{8,11},{9,10},{10,... | collective-permute-start | bytes 2555912 | tf_op jit(solution)/shard_map/ppermute | solution.py:291
  17.9 94.3 %copy-start = (bf16[352,1024]{1,0:T(8,128)(2,1)}, bf16[352,1024]{1,0:T(8,128)(2,1)S(1)}, u32[]{:S(2)}) copy-start(bf16[352,1024]{1,0:T(8,128)(2,1)S(1)} %get-tuple-element.40.refs_2_) | copy-start | bytes 2162692
  17.9 39.7 %collective-permute-start.10 = (bf16[352,1024]{1,0:T(8,128)(2,1)S(1)}, bf16[352,1024]{1,0:T(8,128)(2,1)}, u32[]{:S(2)}, u32[]{:S(2)}) collective-permute-start(bf16[352,1024]{1,0:T(8,128)(2,1)S(1)} %get-tuple-element.40.refs_2_), channel_id=1, source_target_pairs={{0,1},{1,0},{2,3},{3,2},{4,5},{5,4},{6,7},{7,6},{8,9},{9,8},{10,11... | collective-permute-start | bytes 2162696 | tf_op jit(solution)/shard_map/ppermute | solution.py:291
  18.0 26.0 %collective-permute-start.7 = (f32[48,1024]{1,0:T(8,128)S(1)}, f32[48,1024]{1,0:T(8,128)S(1)}, u32[]{:S(2)}, u32[]{:S(2)}) collective-permute-start(f32[48,1024]{1,0:T(8,128)S(1)} %get-tuple-element.35), channel_id=1, source_target_pairs={{0,3},{1,2},{2,1},{3,0},{4,7},{5,6},{6,5},{7,4},{8,11},{9,10},{10,... | collective-permute-start | bytes 589832 | tf_op jit(solution)/shard_map/ppermute | solution.py:291
  18.5 28.2 %collective-permute-start.4 = (bf16[96,1024]{1,0:T(8,128)(2,1)}, bf16[96,1024]{1,0:T(8,128)(2,1)S(1)}, u32[]{:S(2)}, u32[]{:S(2)}) collective-permute-start(bf16[96,1024]{1,0:T(8,128)(2,1)} %get-tuple-element.33.refs_5_), channel_id=1, source_target_pairs={{0,3},{1,2},{2,1},{3,0},{4,7},{5,6},{6,5},{7,4},{8,11},{9,10},{10,... | collective-permute-start | bytes 589832 | tf_op jit(solution)/shard_map/ppermute | solution.py:291
  21.3 22.7 %collective-permute-start.17 = (bf16[16,1024]{1,0:T(8,128)(2,1)}, bf16[16,1024]{1,0:T(8,128)(2,1)}, u32[]{:S(2)}, u32[]{:S(2)}) collective-permute-start(bf16[16,1024]{1,0:T(8,128)(2,1)} %get-tuple-element.42.refs_1_), channel_id=1, source_target_pairs={{0,3},{1,2},{2,1},{3,0},{4,7},{5,6},{6,5},{7,4},{8,11},{9,10},{10,... | collective-permute-start | bytes 98312 | tf_op jit(solution)/shard_map/ppermute | solution.py:291
  44.0 8.0 %collective-permute-start.16 = (bf16[96,1024]{1,0:T(8,128)(2,1)}, bf16[96,1024]{1,0:T(8,128)(2,1)S(1)}, u32[]{:S(2)}, u32[]{:S(2)}) collective-permute-start(bf16[96,1024]{1,0:T(8,128)(2,1)} %get-tuple-element.33.refs_5_), channel_id=1, source_target_pairs={{0,1},{1,0},{2,3},{3,2},{4,5},{5,4},{6,7},{7,6},{8,9},{9,8},{10,11... | collective-permute-start | bytes 589832 | tf_op jit(solution)/shard_map/ppermute | solution.py:291
  44.0 63.1 %collective-permute-start.18 = (bf16[352,1024]{1,0:T(8,128)(2,1)S(1)}, bf16[352,1024]{1,0:T(8,128)(2,1)}, u32[]{:S(2)}, u32[]{:S(2)}) collective-permute-start(bf16[352,1024]{1,0:T(8,128)(2,1)S(1)} %get-tuple-element.40.refs_2_), channel_id=1, source_target_pairs={{0,3},{1,2},{2,1},{3,0},{4,7},{5,6},{6,5},{7,4},{8,11},{9,10},{10,... | collective-permute-start | bytes 2162696 | tf_op jit(solution)/shard_map/ppermute | solution.py:291
  46.7 5.2 %copy-start.2 = (bf16[96,1024]{1,0:T(8,128)(2,1)}, bf16[96,1024]{1,0:T(8,128)(2,1)S(1)}, u32[]{:S(2)}) copy-start(bf16[96,1024]{1,0:T(8,128)(2,1)S(1)} %collective-permute-done.4.refs_5_) | copy-start | bytes 589828
  46.7 10.8 %collective-permute-start.6 = (f32[64,1024]{1,0:T(8,128)S(1)}, f32[64,1024]{1,0:T(8,128)S(1)}, u32[]{:S(2)}, u32[]{:S(2)}) collective-permute-start(f32[64,1024]{1,0:T(8,128)S(1)} %get-tuple-element.34), channel_id=1, source_target_pairs={{0,1},{1,0},{2,3},{3,2},{4,5},{5,4},{6,7},{7,6},{8,9},{9,8},{10,11... | collective-permute-start | bytes 786440 | tf_op jit(solution)/shard_map/ppermute | solution.py:291
  51.9 0.7 copy-start.3
  51.9 58.2 %collective-permute-start.15 = (bf16[416,1024]{1,0:T(8,128)(2,1)}, bf16[416,1024]{1,0:T(8,128)(2,1)}, u32[]{:S(2)}, u32[]{:S(2)}) collective-permute-start(bf16[416,1024]{1,0:T(8,128)(2,1)} %get-tuple-element.41.refs_4_), channel_id=1, source_target_pairs={{0,1},{1,0},{2,3},{3,2},{4,5},{5,4},{6,7},{7,6},{8,9},{9,8},{10,11... | collective-permute-start | bytes 2555912 | tf_op jit(solution)/shard_map/ppermute | solution.py:291
  52.6 68.7 %collective-permute-start.13 = (bf16[416,1024]{1,0:T(8,128)(2,1)}, bf16[416,1024]{1,0:T(8,128)(2,1)S(1)}, u32[]{:S(2)}, u32[]{:S(2)}) collective-permute-start(bf16[416,1024]{1,0:T(8,128)(2,1)} %collective-permute-done.12.refs_4_), channel_id=1, source_target_pairs={{0,1},{1,0},{2,3},{3,2},{4,5},{5,4},{6,7},{7,6},{8,9},{9,8},{10,11... | collective-permute-start | bytes 2555912 | tf_op jit(solution)/shard_map/ppermute | solution.py:291
  57.6 36.6 %collective-permute-start.2 = (bf16[96,1024]{1,0:T(8,128)(2,1)}, bf16[96,1024]{1,0:T(8,128)(2,1)}, u32[]{:S(2)}, u32[]{:S(2)}) collective-permute-start(bf16[96,1024]{1,0:T(8,128)(2,1)} %get-tuple-element.32.refs_3_), channel_id=1, source_target_pairs={{0,1},{1,0},{2,3},{3,2},{4,5},{5,4},{6,7},{7,6},{8,9},{9,8},{10,11... | collective-permute-start | bytes 589832 | tf_op jit(solution)/shard_map/ppermute | solution.py:291
  57.6 63.7 %collective-permute-start.11 = (bf16[352,1024]{1,0:T(8,128)(2,1)}, bf16[352,1024]{1,0:T(8,128)(2,1)S(1)}, u32[]{:S(2)}, u32[]{:S(2)}) collective-permute-start(bf16[352,1024]{1,0:T(8,128)(2,1)} %collective-permute-done.10.refs_2_), channel_id=1, source_target_pairs={{0,3},{1,2},{2,1},{3,0},{4,7},{5,6},{6,5},{7,4},{8,11},{9,10},{10,... | collective-permute-start | bytes 2162696 | tf_op jit(solution)/shard_map/ppermute | solution.py:291
  61.1 56.6 %all-to-all-start = ((bf16[64,16,128]{2,1,0:T(8,128)(2,1)}), bf16[64,16,128]{2,1,0:T(8,128)(2,1)S(1)}, u32[]{:S(2)}, u32[]{:S(2)}) async-start(bf16[64,16,128]{2,1,0:T(8,128)(2,1)} %router.1), calls=%async_computation | async-start | bytes 524288 | tf_op jit(solution)/shard_map/all_to_all | solution.py:318
  94.2 7.4 %collective-permute-start.14 = (bf16[96,1024]{1,0:T(8,128)(2,1)}, bf16[96,1024]{1,0:T(8,128)(2,1)S(1)}, u32[]{:S(2)}, u32[]{:S(2)}) collective-permute-start(bf16[96,1024]{1,0:T(8,128)(2,1)} %get-tuple-element.32.refs_3_), channel_id=1, source_target_pairs={{0,3},{1,2},{2,1},{3,0},{4,7},{5,6},{6,5},{7,4},{8,11},{9,10},{10,... | collective-permute-start | bytes 589832 | tf_op jit(solution)/shard_map/ppermute | solution.py:291
  96.8 18.5 %copy-start.5 = (bf16[16,1024]{1,0:T(8,128)(2,1)}, bf16[16,1024]{1,0:T(8,128)(2,1)S(1)}, u32[]{:S(2)}) copy-start(bf16[16,1024]{1,0:T(8,128)(2,1)S(1)} %divide_convert_fusion.2.refs_1_) | copy-start | bytes 98308
  101.6 2.6 %copy-start.4 = (bf16[96,1024]{1,0:T(8,128)(2,1)}, bf16[96,1024]{1,0:T(8,128)(2,1)S(1)}, u32[]{:S(2)}) copy-start(bf16[96,1024]{1,0:T(8,128)(2,1)S(1)} %collective-permute-done.14.refs_1_) | copy-start | bytes 589828
  101.6 5.4 %collective-permute-start.9 = (bf16[16,1024]{1,0:T(8,128)(2,1)S(1)}, bf16[16,1024]{1,0:T(8,128)(2,1)S(1)}, u32[]{:S(2)}, u32[]{:S(2)}) collective-permute-start(bf16[16,1024]{1,0:T(8,128)(2,1)S(1)} %divide_convert_fusion.2.refs_1_), channel_id=1, source_target_pairs={{0,3},{1,2},{2,1},{3,0},{4,7},{5,6},{6,5},{7,4},{8,11},{9,10},{10,... | collective-permute-start | bytes 98312 | tf_op jit(solution)/shard_map/ppermute | solution.py:291
  107.0 15.6 %collective-permute-start.5 = (bf16[96,1024]{1,0:T(8,128)(2,1)}, bf16[96,1024]{1,0:T(8,128)(2,1)S(1)}, u32[]{:S(2)}, u32[]{:S(2)}) collective-permute-start(bf16[96,1024]{1,0:T(8,128)(2,1)} %copy-done.2), channel_id=1, source_target_pairs={{0,1},{1,0},{2,3},{3,2},{4,5},{5,4},{6,7},{7,6},{8,9},{9,8},{10,11... | collective-permute-start | bytes 589832 | tf_op jit(solution)/shard_map/ppermute | solution.py:291
  107.0 15.6 %collective-permute-start.3 = (bf16[96,1024]{1,0:T(8,128)(2,1)}, bf16[96,1024]{1,0:T(8,128)(2,1)S(1)}, u32[]{:S(2)}, u32[]{:S(2)}) collective-permute-start(bf16[96,1024]{1,0:T(8,128)(2,1)} %collective-permute-done.2.refs_0_), channel_id=1, source_target_pairs={{0,3},{1,2},{2,1},{3,0},{4,7},{5,6},{6,5},{7,4},{8,11},{9,10},{10,... | collective-permute-start | bytes 589832 | tf_op jit(solution)/shard_map/ppermute | solution.py:291
  110.1 5.2 %copy-start.1 = (bf16[48,1024]{1,0:T(8,128)(2,1)}, bf16[48,1024]{1,0:T(8,128)(2,1)S(1)}, u32[]{:S(2)}) copy-start(bf16[48,1024]{1,0:T(8,128)(2,1)S(1)} %get-tuple-element.56.refs_3_) | copy-start | bytes 294916
  110.1 11.2 %collective-permute-start.8 = (bf16[48,1024]{1,0:T(8,128)(2,1)S(1)}, bf16[48,1024]{1,0:T(8,128)(2,1)S(1)}, u32[]{:S(2)}, u32[]{:S(2)}) collective-permute-start(bf16[48,1024]{1,0:T(8,128)(2,1)S(1)} %get-tuple-element.56.refs_3_), channel_id=1, source_target_pairs={{0,1},{1,0},{2,3},{3,2},{4,5},{5,4},{6,7},{7,6},{8,9},{9,8},{10,11... | collective-permute-start | bytes 294920 | tf_op jit(solution)/shard_map/ppermute | solution.py:291

commit v4 on v3

--- a/solution.py
+++ b/solution.py
@@ -10,7 +10,7 @@
 
 RAW_NEAR, RAW_WIDE = 64, 48
 GATE_LAST, UP_LAST = 96, 96
-STEP = 64
+STEPS = (512,), (256, 192, 64)
 LANES = 128
 VMEM = pl.BlockSpec(memory_space=pltpu.VMEM)
 ANY = pl.BlockSpec(memory_space=pl.ANY)
@@ -25,12 +25,11 @@
 
 
 def sums_kernel(train_gate, other_gate, train_up, other_up, weight, gain, small, raw_near, raw_wide, gate, up, train, other, router, sems):
-    rows, cols = up.shape
-    steps = rows // STEP
+    cols = up.shape[1]
     sources = ((train_gate, other_gate), (train_up, other_up))
 
     def copies(k, i):
-        at = pl.ds(i * STEP, STEP)
+        at = pl.ds(sum(STEPS[k][:i]), STEPS[k][i])
         return [
             pltpu.make_async_copy(hbm.at[at], held.at[k, at], sems.at[k, i])
             for hbm, held in zip(sources[k], (train, other))
@@ -38,7 +37,7 @@
 
     rest = [pltpu.make_async_copy(v, router.at[k], sems.at[2, k]) for k, v in enumerate((weight, gain))]
     for k in range(2):
-        for i in range(steps):
+        for i in range(len(STEPS[k])):
             for c in copies(k, i):
                 c.start()
         if k == 0:
@@ -47,11 +46,11 @@
     small[2:] = jnp.zeros((small.shape[0] - 2, cols), jnp.float32)
     for k in range(2):
         total = jnp.zeros((8, cols), jnp.float32)
-        for i in range(steps):
+        for i, size in enumerate(STEPS[k]):
             for c in copies(k, i):
                 c.wait()
-
-            for row in range(i * STEP, (i + 1) * STEP, 16):
+            start = sum(STEPS[k][:i])
+            for row in range(start, start + size, 16):
                 v = train[k, row : row + 16, :] + other[k, row : row + 16, :].astype(jnp.float32)
                 total += v[:8] * v[:8] + v[8:] * v[8:]
                 for ref, first in ((up, 0),) if k else ((raw_near, 0), (raw_wide, 0), (gate, RAW_NEAR)):
@@ -81,7 +80,7 @@
             pltpu.VMEM((2, rows, cols), f32),
             pltpu.VMEM((2, rows, cols), jnp.bfloat16),
             pltpu.VMEM((2, *args[4].shape), f32),
-            pltpu.SemaphoreType.DMA((3, rows // STEP)),
+            pltpu.SemaphoreType.DMA((3, max(map(len, STEPS)))),
         ],
         compiler_params=pltpu.CompilerParams(vmem_limit_bytes=20 << 20),
         name="sums",

time: 124 us -> 124 us (level)
  no operation moved by 1% of the time
where the time goes in v4:
time: 124 us; the launch traced here: 123 us
  waiting for transfers between devices  64.1 us (52%)
  starting transfers between devices  38.9 us (31%)
  Pallas kernels  16.1 us (13%)
  local copies, waits for them, and re-layouts  2.66 us (2%)
    ppermute x19, waiting for transfers between devices, exchanged(): return lax.ppermute(value, 'fsdp', [(i, i ^ flip) for i in range(n)])  64.1 us
    ppermute x19, starting transfers between devices, exchanged(): return lax.ppermute(value, 'fsdp', [(i, i ^ flip) for i in range(n)])  28.5 us
    all_to_all x1, starting transfers between devices, body(): lax.all_to_all(copies, 'ep', split_axis=0, concat_axis=0, tiled=True)  10.5 us
    pallas_call x5, Pallas kernels, place(): pl.pallas_call(functools.partial(place_kernel, rows, len(used), spots), o...  9.82 us
    pallas_call x1, Pallas kernels, sums(): pl.pallas_call(sums_kernel, out_shape=(pltpu.VMEM((4, cols), f32), pltpu....  2.92 us
    unnamed x15, local copies, waits for them, and re-layouts  2.66 us
  transfers between devices with their start and end apart: 20, of which 8 were waited for; matrix products, arithmetic and copies ran while one was open for 2% of the time, Pallas kernels for 8%

profile of v4, /device:TPU:128, one launch (start us, length us, event | category | flops | bytes accessed | tf_op | source)
XLA Modules:
  0.0 123.3 jit_solution(7786139555457857804)
XLA Ops:
  0.6 2.9 %sums.1 = (f32[4,1024]{1,0:T(4,128)S(1)}, f32[64,1024]{1,0:T(8,128)S(1)}, f32[48,1024]{1,0:T(8,128)S(1)}, f32[352,1024]{1,0:T(8,128)S(1)}, f32[512,1024]{1,0:T(8,128)S(1)}) custom-call(f32[512,1024]{1,0:T(8,128)} %bitcast.20, bf16[512,1024]{1,0:T(8,128)(2,1)} %bitcast.22, f32[512,1024]{1,0:T(8,128)} %bitcast.24, bf16[512,1024]{1,0:T(8,128)(2,1)} %bitcast.26, ...), custom_call_target="tpu_custom_call" | custom-call | flops 4194304 | bytes 6291456 | tf_op jit(solution)/shard_map/sums/pallas_call | solution.py:68
  3.6 1.6 %collective-permute-start = (f32[4,1024]{1,0:T(4,128)S(1)}, f32[4,1024]{1,0:T(4,128)S(1)}, u32[]{:S(2)}, u32[]{:S(2)}) collective-permute-start(f32[4,1024]{1,0:T(4,128)S(1)} %get-tuple-element.30.own), channel_id=1, source_target_pairs={{0,1},{1,0},{2,3},{3,2},{4,5},{5,4},{6,7},{7,6},{8,9},{9,8},{10,11... | collective-permute-start | bytes 49160 | tf_op jit(solution)/shard_map/ppermute | solution.py:290
  5.1 2.2 %collective-permute-done.near = f32[4,1024]{1,0:T(4,128)S(1)} collective-permute-done((f32[4,1024]{1,0:T(4,128)S(1)}, f32[4,1024]{1,0:T(4,128)S(1)}, u32[]{:S(2)}, u32[]{:S(2)}) %collective-permute-start) | collective-permute-done | bytes 16416 | tf_op jit(solution)/shard_map/ppermute | solution.py:290
  7.4 2.8 %collective-permute-start.1 = (f32[4,1024]{1,0:T(4,128)S(1)}, f32[4,1024]{1,0:T(4,128)S(1)}, u32[]{:S(2)}, u32[]{:S(2)}) collective-permute-start(f32[4,1024]{1,0:T(4,128)S(1)} %pair.1), channel_id=1, source_target_pairs={{0,3},{1,2},{2,1},{3,0},{4,7},{5,6},{6,5},{7,4},{8,11},{9,10},{10,... | collective-permute-start | bytes 49160 | tf_op jit(solution)/shard_map/ppermute | solution.py:290
  10.1 2.2 %collective-permute-done.1.wide = f32[4,1024]{1,0:T(4,128)S(1)} collective-permute-done((f32[4,1024]{1,0:T(4,128)S(1)}, f32[4,1024]{1,0:T(4,128)S(1)}, u32[]{:S(2)}, u32[]{:S(2)}) %collective-permute-start.1) | collective-permute-done | bytes 16416 | tf_op jit(solution)/shard_map/ppermute | solution.py:290
  12.3 2.4 %ready_rest.1 = (bf16[416,1024]{1,0:T(8,128)(2,1)}, bf16[96,1024]{1,0:T(8,128)(2,1)}, bf16[96,1024]{1,0:T(8,128)(2,1)}, bf16[48,1024]{1,0:T(8,128)(2,1)}, bf16[1...) custom-call(f32[4,1024]{1,0:T(4,128)S(1)} %pair.1, f32[4,1024]{1,0:T(4,128)S(1)} %collective-permute-done.1.wide, ...), custom_call_target="tpu_custom_call" | custom-call | flops 1572864 | bytes 1572864 | tf_op jit(solution)/shard_map/ready_rest/pallas_call | solution.py:173
  14.7 2.8 %collective-permute-start.12 = (bf16[416,1024]{1,0:T(8,128)(2,1)}, bf16[416,1024]{1,0:T(8,128)(2,1)}, u32[]{:S(2)}, u32[]{:S(2)}) collective-permute-start(bf16[416,1024]{1,0:T(8,128)(2,1)} %get-tuple-element.41.refs_4_), channel_id=1, source_target_pairs={{0,3},{1,2},{2,1},{3,0},{4,7},{5,6},{6,5},{7,4},{8,11},{9,10},{10,... | collective-permute-start | bytes 2555912 | tf_op jit(solution)/shard_map/ppermute | solution.py:290
  17.6 0.2 ready_first.1
  17.7 0.0 copy-start
  17.8 0.1 collective-permute-start.10
  17.9 0.6 collective-permute-start.7
  18.4 2.8 %collective-permute-start.4 = (bf16[96,1024]{1,0:T(8,128)(2,1)}, bf16[96,1024]{1,0:T(8,128)(2,1)S(1)}, u32[]{:S(2)}, u32[]{:S(2)}) collective-permute-start(bf16[96,1024]{1,0:T(8,128)(2,1)} %get-tuple-element.33.refs_5_), channel_id=1, source_target_pairs={{0,3},{1,2},{2,1},{3,0},{4,7},{5,6},{6,5},{7,4},{8,11},{9,10},{10,... | collective-permute-start | bytes 589832 | tf_op jit(solution)/shard_map/ppermute | solution.py:290
  21.2 0.5 collective-permute-start.17
  21.7 22.2 %collective-permute-done.17.refs_4_ = bf16[16,1024]{1,0:T(8,128)(2,1)} collective-permute-done((bf16[16,1024]{1,0:T(8,128)(2,1)}, bf16[16,1024]{1,0:T(8,128)(2,1)}, u32[]{:S(2)}, u32[]{:S(2)}) %collective-permute-start.17) | collective-permute-done | bytes 32800 | tf_op jit(solution)/shard_map/ppermute | solution.py:290
  43.8 0.0 collective-permute-start.16
  43.8 0.0 collective-permute-done.7
  43.8 2.8 %collective-permute-start.18 = (bf16[352,1024]{1,0:T(8,128)(2,1)S(1)}, bf16[352,1024]{1,0:T(8,128)(2,1)}, u32[]{:S(2)}, u32[]{:S(2)}) collective-permute-start(bf16[352,1024]{1,0:T(8,128)(2,1)S(1)} %get-tuple-element.40.refs_2_), channel_id=1, source_target_pairs={{0,3},{1,2},{2,1},{3,0},{4,7},{5,6},{6,5},{7,4},{8,11},{9,10},{10,... | collective-permute-start | bytes 2162696 | tf_op jit(solution)/shard_map/ppermute | solution.py:290
  46.6 0.0 collective-permute-done.4.refs_5_
  46.6 0.0 copy-start.2
  46.6 1.4 %collective-permute-start.6 = (f32[64,1024]{1,0:T(8,128)S(1)}, f32[64,1024]{1,0:T(8,128)S(1)}, u32[]{:S(2)}, u32[]{:S(2)}) collective-permute-start(f32[64,1024]{1,0:T(8,128)S(1)} %get-tuple-element.34), channel_id=1, source_target_pairs={{0,1},{1,0},{2,3},{3,2},{4,5},{5,4},{6,7},{7,6},{8,9},{9,8},{10,11... | collective-permute-start | bytes 786440 | tf_op jit(solution)/shard_map/ppermute | solution.py:290
  48.0 3.8 %collective-permute-done.16.refs_3_ = bf16[96,1024]{1,0:T(8,128)(2,1)S(1)} collective-permute-done((bf16[96,1024]{1,0:T(8,128)(2,1)}, bf16[96,1024]{1,0:T(8,128)(2,1)S(1)}, u32[]{:S(2)}, u32[]{:S(2)}) %collective-permute-start.16) | collective-permute-done | bytes 196640 | tf_op jit(solution)/shard_map/ppermute | solution.py:290
  51.8 0.0 copy-start.3
  51.8 0.0 collective-permute-start.15
  51.8 0.0 copy-done.2
  51.8 0.7 copy-done.3
  52.5 0.0 collective-permute-done.12.refs_4_
  52.5 1.4 %collective-permute-start.13 = (bf16[416,1024]{1,0:T(8,128)(2,1)}, bf16[416,1024]{1,0:T(8,128)(2,1)S(1)}, u32[]{:S(2)}, u32[]{:S(2)}) collective-permute-start(bf16[416,1024]{1,0:T(8,128)(2,1)} %collective-permute-done.12.refs_4_), channel_id=1, source_target_pairs={{0,1},{1,0},{2,3},{3,2},{4,5},{5,4},{6,7},{7,6},{8,9},{9,8},{10,11... | collective-permute-start | bytes 2555912 | tf_op jit(solution)/shard_map/ppermute | solution.py:290
  53.9 3.5 %collective-permute-done.6 = f32[64,1024]{1,0:T(8,128)S(1)} collective-permute-done((f32[64,1024]{1,0:T(8,128)S(1)}, f32[64,1024]{1,0:T(8,128)S(1)}, u32[]{:S(2)}, u32[]{:S(2)}) %collective-permute-start.6) | collective-permute-done | bytes 262176 | tf_op jit(solution)/shard_map/ppermute | solution.py:290
  57.4 0.0 collective-permute-start.2
  57.4 0.0 collective-permute-done.10.refs_2_
  57.4 2.8 %collective-permute-start.11 = (bf16[352,1024]{1,0:T(8,128)(2,1)}, bf16[352,1024]{1,0:T(8,128)(2,1)S(1)}, u32[]{:S(2)}, u32[]{:S(2)}) collective-permute-start(bf16[352,1024]{1,0:T(8,128)(2,1)} %collective-permute-done.10.refs_2_), channel_id=1, source_target_pairs={{0,3},{1,2},{2,1},{3,0},{4,7},{5,6},{6,5},{7,4},{8,11},{9,10},{10,... | collective-permute-start | bytes 2162696 | tf_op jit(solution)/shard_map/ppermute | solution.py:290
  60.2 0.8 router.1
  61.0 10.5 %all-to-all-start = ((bf16[64,16,128]{2,1,0:T(8,128)(2,1)}), bf16[64,16,128]{2,1,0:T(8,128)(2,1)S(1)}, u32[]{:S(2)}, u32[]{:S(2)}) async-start(bf16[64,16,128]{2,1,0:T(8,128)(2,1)} %router.1), calls=%async_computation | async-start | bytes 524288 | tf_op jit(solution)/shard_map/all_to_all | solution.py:317
  71.5 22.6 %collective-permute-done.2.refs_0_ = bf16[96,1024]{1,0:T(8,128)(2,1)} collective-permute-done((bf16[96,1024]{1,0:T(8,128)(2,1)}, bf16[96,1024]{1,0:T(8,128)(2,1)}, u32[]{:S(2)}, u32[]{:S(2)}) %collective-permute-start.2) | collective-permute-done | bytes 196640 | tf_op jit(solution)/shard_map/ppermute | solution.py:290
  94.1 2.6 %collective-permute-start.14 = (bf16[96,1024]{1,0:T(8,128)(2,1)}, bf16[96,1024]{1,0:T(8,128)(2,1)S(1)}, u32[]{:S(2)}, u32[]{:S(2)}) collective-permute-start(bf16[96,1024]{1,0:T(8,128)(2,1)} %get-tuple-element.32.refs_3_), channel_id=1, source_target_pairs={{0,3},{1,2},{2,1},{3,0},{4,7},{5,6},{6,5},{7,4},{8,11},{9,10},{10,... | collective-permute-start | bytes 589832 | tf_op jit(solution)/shard_map/ppermute | solution.py:290
  96.7 0.0 copy-start.5
  96.7 4.8 %collective-permute-done.14.refs_1_ = bf16[96,1024]{1,0:T(8,128)(2,1)S(1)} collective-permute-done((bf16[96,1024]{1,0:T(8,128)(2,1)}, bf16[96,1024]{1,0:T(8,128)(2,1)S(1)}, u32[]{:S(2)}, u32[]{:S(2)}) %collective-permute-start.14) | collective-permute-done | bytes 196640 | tf_op jit(solution)/shard_map/ppermute | solution.py:290
  101.5 0.0 copy-start.4
  101.5 2.6 %collective-permute-start.9 = (bf16[16,1024]{1,0:T(8,128)(2,1)S(1)}, bf16[16,1024]{1,0:T(8,128)(2,1)S(1)}, u32[]{:S(2)}, u32[]{:S(2)}) collective-permute-start(bf16[16,1024]{1,0:T(8,128)(2,1)S(1)} %divide_convert_fusion.2.refs_1_), channel_id=1, source_target_pairs={{0,3},{1,2},{2,1},{3,0},{4,7},{5,6},{6,5},{7,4},{8,11},{9,10},{10,... | collective-permute-start | bytes 98312 | tf_op jit(solution)/shard_map/ppermute | solution.py:290
  104.1 0.0 copy-done.4
  104.1 2.8 %collective-permute-done.9.refs_1_ = bf16[16,1024]{1,0:T(8,128)(2,1)S(1)} collective-permute-done((bf16[16,1024]{1,0:T(8,128)(2,1)S(1)}, bf16[16,1024]{1,0:T(8,128)(2,1)S(1)}, u32[]{:S(2)}, u32[]{:S(2)}) %collective-permute-start.9) | collective-permute-done | bytes 32800 | tf_op jit(solution)/shard_map/ppermute | solution.py:290
  106.9 0.0 collective-permute-start.5
  106.9 0.0 collective-permute-done.18.refs_5_
  106.9 2.4 %collective-permute-start.3 = (bf16[96,1024]{1,0:T(8,128)(2,1)}, bf16[96,1024]{1,0:T(8,128)(2,1)S(1)}, u32[]{:S(2)}, u32[]{:S(2)}) collective-permute-start(bf16[96,1024]{1,0:T(8,128)(2,1)} %collective-permute-done.2.refs_0_), channel_id=1, source_target_pairs={{0,3},{1,2},{2,1},{3,0},{4,7},{5,6},{6,5},{7,4},{8,11},{9,10},{10,... | collective-permute-start | bytes 589832 | tf_op jit(solution)/shard_map/ppermute | solution.py:290
  109.3 0.7 divide_convert_fusion
  110.0 0.0 collective-permute-done.15.refs_2_
  110.0 1.4 %collective-permute-start.8 = (bf16[48,1024]{1,0:T(8,128)(2,1)S(1)}, bf16[48,1024]{1,0:T(8,128)(2,1)S(1)}, u32[]{:S(2)}, u32[]{:S(2)}) collective-permute-start(bf16[48,1024]{1,0:T(8,128)(2,1)S(1)} %get-tuple-element.56.refs_3_), channel_id=1, source_target_pairs={{0,1},{1,0},{2,3},{3,2},{4,5},{5,4},{6,7},{7,6},{8,9},{9,8},{10,11... | collective-permute-start | bytes 294920 | tf_op jit(solution)/shard_map/ppermute | solution.py:290
  111.4 0.6 copy.28
  112.0 0.0 copy-done
  112.0 2.6 %place.5 = (bf16[2048,1024]{1,0:T(8,128)(2,1)}, bf16[2048,1024]{1,0:T(8,128)(2,1)}) custom-call(bf16[48,1024]{1,0:T(8,128)(2,1)} %get-tuple-element.43.refs_0_, bf16[16,1024]{1,0:T(8,128)(2,1)} %get-tuple-element.42.refs_1_, bf16[352,1024]{1,0:T(8,128)(2,1)} %copy-done, bf16[96,1024]{1,0:T(8,128)(2,1)} %get-tuple-element.32.refs_3_, ...), custom_call_target="tpu_custom_call" | custom-call | bytes 4194304 | tf_op jit(solution)/shard_map/place/pallas_call | solution.py:262
  114.6 0.6 copy.29
  115.2 0.0 copy-done.5
  115.2 0.0 copy-done.1
  115.2 2.4 %place.6.refs_6_ = bf16[2048,1024]{1,0:T(8,128)(2,1)} custom-call(bf16[48,1024]{1,0:T(8,128)(2,1)} %get-tuple-element.55.refs_0_, bf16[16,1024]{1,0:T(8,128)(2,1)} %copy-done.5, bf16[352,1024]{1,0:T(8,128)(2,1)} %collective-permute-done.10.refs_2_, bf16[48,1024]{1,0:T(8,128)(2,1)} %copy-done.1, ...), custom_call_target="tpu_custom_call", output_to_operand_aliasing={{}: (6, {})} | custom-call | bytes 3407872 | tf_op jit(solution)/shard_map/place/pallas_call | solution.py:262
  117.6 0.0 all-to-all-done
  117.6 0.8 copy.20
  118.4 2.8 %place.7 = (bf16[2048,1024]{1,0:T(8,128)(2,1)}, bf16[2048,1024]{1,0:T(8,128)(2,1)}) custom-call(bf16[96,1024]{1,0:T(8,128)(2,1)} %collective-permute-done.2.refs_0_, bf16[96,1024]{1,0:T(8,128)(2,1)} %copy-done.4, bf16[416,1024]{1,0:T(8,128)(2,1)} %collective-permute-done.15.refs_2_, ...), custom_call_target="tpu_custom_call", output_to_operand_aliasing={{0}: (6, {}), {1}: (7, {})} | custom-call | bytes 4980736 | tf_op jit(solution)/shard_map/place/pallas_call | solution.py:262
  121.2 0.0 collective-permute-done.8.refs_0_
  121.2 0.0 collective-permute-done.11.refs_2_
  121.2 0.0 collective-permute-done.13.refs_3_
  121.2 1.3 %place.8 = (bf16[2048,1024]{1,0:T(8,128)(2,1)}, bf16[2048,1024]{1,0:T(8,128)(2,1)}) custom-call(bf16[48,1024]{1,0:T(8,128)(2,1)S(1)} %collective-permute-done.8.refs_0_, bf16[16,1024]{1,0:T(8,128)(2,1)S(1)} %collective-permute-done.9.refs_1_, bf16[352,1024]{1,0:T(8,128)(2,1)S(1)} %collective-permute-done.11.refs_2_, ...), custom_call_target="tpu_custom_call", output_to_operand_aliasing={{0}: (4, {}), {1}: (5, {})} | custom-call | bytes 3407872 | tf_op jit(solution)/shard_map/place/pallas_call | solution.py:262
  122.5 0.0 collective-permute-done.5.refs_1_
  122.5 0.0 collective-permute-done.3.refs_0_
  122.5 0.8 place.9
  (3 shorter events, 0.0 us)
Async XLA Ops:
  3.6 3.8 %collective-permute-start = (f32[4,1024]{1,0:T(4,128)S(1)}, f32[4,1024]{1,0:T(4,128)S(1)}, u32[]{:S(2)}, u32[]{:S(2)}) collective-permute-start(f32[4,1024]{1,0:T(4,128)S(1)} %get-tuple-element.30.own), channel_id=1, source_target_pairs={{0,1},{1,0},{2,3},{3,2},{4,5},{5,4},{6,7},{7,6},{8,9},{9,8},{10,11... | collective-permute-start | bytes 49160 | tf_op jit(solution)/shard_map/ppermute | solution.py:290
  7.4 4.9 %collective-permute-start.1 = (f32[4,1024]{1,0:T(4,128)S(1)}, f32[4,1024]{1,0:T(4,128)S(1)}, u32[]{:S(2)}, u32[]{:S(2)}) collective-permute-start(f32[4,1024]{1,0:T(4,128)S(1)} %pair.1), channel_id=1, source_target_pairs={{0,3},{1,2},{2,1},{3,0},{4,7},{5,6},{6,5},{7,4},{8,11},{9,10},{10,... | collective-permute-start | bytes 49160 | tf_op jit(solution)/shard_map/ppermute | solution.py:290
  14.7 37.8 %collective-permute-start.12 = (bf16[416,1024]{1,0:T(8,128)(2,1)}, bf16[416,1024]{1,0:T(8,128)(2,1)}, u32[]{:S(2)}, u32[]{:S(2)}) collective-permute-start(bf16[416,1024]{1,0:T(8,128)(2,1)} %get-tuple-element.41.refs_4_), channel_id=1, source_target_pairs={{0,3},{1,2},{2,1},{3,0},{4,7},{5,6},{6,5},{7,4},{8,11},{9,10},{10,... | collective-permute-start | bytes 2555912 | tf_op jit(solution)/shard_map/ppermute | solution.py:290
  17.7 94.3 %copy-start = (bf16[352,1024]{1,0:T(8,128)(2,1)}, bf16[352,1024]{1,0:T(8,128)(2,1)S(1)}, u32[]{:S(2)}) copy-start(bf16[352,1024]{1,0:T(8,128)(2,1)S(1)} %get-tuple-element.40.refs_2_) | copy-start | bytes 2162692
  17.8 39.7 %collective-permute-start.10 = (bf16[352,1024]{1,0:T(8,128)(2,1)S(1)}, bf16[352,1024]{1,0:T(8,128)(2,1)}, u32[]{:S(2)}, u32[]{:S(2)}) collective-permute-start(bf16[352,1024]{1,0:T(8,128)(2,1)S(1)} %get-tuple-element.40.refs_2_), channel_id=1, source_target_pairs={{0,1},{1,0},{2,3},{3,2},{4,5},{5,4},{6,7},{7,6},{8,9},{9,8},{10,11... | collective-permute-start | bytes 2162696 | tf_op jit(solution)/shard_map/ppermute | solution.py:290
  17.9 26.0 %collective-permute-start.7 = (f32[48,1024]{1,0:T(8,128)S(1)}, f32[48,1024]{1,0:T(8,128)S(1)}, u32[]{:S(2)}, u32[]{:S(2)}) collective-permute-start(f32[48,1024]{1,0:T(8,128)S(1)} %get-tuple-element.35), channel_id=1, source_target_pairs={{0,3},{1,2},{2,1},{3,0},{4,7},{5,6},{6,5},{7,4},{8,11},{9,10},{10,... | collective-permute-start | bytes 589832 | tf_op jit(solution)/shard_map/ppermute | solution.py:290
  18.4 28.2 %collective-permute-start.4 = (bf16[96,1024]{1,0:T(8,128)(2,1)}, bf16[96,1024]{1,0:T(8,128)(2,1)S(1)}, u32[]{:S(2)}, u32[]{:S(2)}) collective-permute-start(bf16[96,1024]{1,0:T(8,128)(2,1)} %get-tuple-element.33.refs_5_), channel_id=1, source_target_pairs={{0,3},{1,2},{2,1},{3,0},{4,7},{5,6},{6,5},{7,4},{8,11},{9,10},{10,... | collective-permute-start | bytes 589832 | tf_op jit(solution)/shard_map/ppermute | solution.py:290
  21.2 22.7 %collective-permute-start.17 = (bf16[16,1024]{1,0:T(8,128)(2,1)}, bf16[16,1024]{1,0:T(8,128)(2,1)}, u32[]{:S(2)}, u32[]{:S(2)}) collective-permute-start(bf16[16,1024]{1,0:T(8,128)(2,1)} %get-tuple-element.42.refs_1_), channel_id=1, source_target_pairs={{0,3},{1,2},{2,1},{3,0},{4,7},{5,6},{6,5},{7,4},{8,11},{9,10},{10,... | collective-permute-start | bytes 98312 | tf_op jit(solution)/shard_map/ppermute | solution.py:290
  43.8 8.0 %collective-permute-start.16 = (bf16[96,1024]{1,0:T(8,128)(2,1)}, bf16[96,1024]{1,0:T(8,128)(2,1)S(1)}, u32[]{:S(2)}, u32[]{:S(2)}) collective-permute-start(bf16[96,1024]{1,0:T(8,128)(2,1)} %get-tuple-element.33.refs_5_), channel_id=1, source_target_pairs={{0,1},{1,0},{2,3},{3,2},{4,5},{5,4},{6,7},{7,6},{8,9},{9,8},{10,11... | collective-permute-start | bytes 589832 | tf_op jit(solution)/shard_map/ppermute | solution.py:290
  43.8 63.1 %collective-permute-start.18 = (bf16[352,1024]{1,0:T(8,128)(2,1)S(1)}, bf16[352,1024]{1,0:T(8,128)(2,1)}, u32[]{:S(2)}, u32[]{:S(2)}) collective-permute-start(bf16[352,1024]{1,0:T(8,128)(2,1)S(1)} %get-tuple-element.40.refs_2_), channel_id=1, source_target_pairs={{0,3},{1,2},{2,1},{3,0},{4,7},{5,6},{6,5},{7,4},{8,11},{9,10},{10,... | collective-permute-start | bytes 2162696 | tf_op jit(solution)/shard_map/ppermute | solution.py:290
  46.6 5.2 %copy-start.2 = (bf16[96,1024]{1,0:T(8,128)(2,1)}, bf16[96,1024]{1,0:T(8,128)(2,1)S(1)}, u32[]{:S(2)}) copy-start(bf16[96,1024]{1,0:T(8,128)(2,1)S(1)} %collective-permute-done.4.refs_5_) | copy-start | bytes 589828
  46.6 10.8 %collective-permute-start.6 = (f32[64,1024]{1,0:T(8,128)S(1)}, f32[64,1024]{1,0:T(8,128)S(1)}, u32[]{:S(2)}, u32[]{:S(2)}) collective-permute-start(f32[64,1024]{1,0:T(8,128)S(1)} %get-tuple-element.34), channel_id=1, source_target_pairs={{0,1},{1,0},{2,3},{3,2},{4,5},{5,4},{6,7},{7,6},{8,9},{9,8},{10,11... | collective-permute-start | bytes 786440 | tf_op jit(solution)/shard_map/ppermute | solution.py:290
  51.8 0.7 copy-start.3
  51.8 58.2 %collective-permute-start.15 = (bf16[416,1024]{1,0:T(8,128)(2,1)}, bf16[416,1024]{1,0:T(8,128)(2,1)}, u32[]{:S(2)}, u32[]{:S(2)}) collective-permute-start(bf16[416,1024]{1,0:T(8,128)(2,1)} %get-tuple-element.41.refs_4_), channel_id=1, source_target_pairs={{0,1},{1,0},{2,3},{3,2},{4,5},{5,4},{6,7},{7,6},{8,9},{9,8},{10,11... | collective-permute-start | bytes 2555912 | tf_op jit(solution)/shard_map/ppermute | solution.py:290
  52.5 68.7 %collective-permute-start.13 = (bf16[416,1024]{1,0:T(8,128)(2,1)}, bf16[416,1024]{1,0:T(8,128)(2,1)S(1)}, u32[]{:S(2)}, u32[]{:S(2)}) collective-permute-start(bf16[416,1024]{1,0:T(8,128)(2,1)} %collective-permute-done.12.refs_4_), channel_id=1, source_target_pairs={{0,1},{1,0},{2,3},{3,2},{4,5},{5,4},{6,7},{7,6},{8,9},{9,8},{10,11... | collective-permute-start | bytes 2555912 | tf_op jit(solution)/shard_map/ppermute | solution.py:290
  57.4 36.6 %collective-permute-start.2 = (bf16[96,1024]{1,0:T(8,128)(2,1)}, bf16[96,1024]{1,0:T(8,128)(2,1)}, u32[]{:S(2)}, u32[]{:S(2)}) collective-permute-start(bf16[96,1024]{1,0:T(8,128)(2,1)} %get-tuple-element.32.refs_3_), channel_id=1, source_target_pairs={{0,1},{1,0},{2,3},{3,2},{4,5},{5,4},{6,7},{7,6},{8,9},{9,8},{10,11... | collective-permute-start | bytes 589832 | tf_op jit(solution)/shard_map/ppermute | solution.py:290
  57.4 63.7 %collective-permute-start.11 = (bf16[352,1024]{1,0:T(8,128)(2,1)}, bf16[352,1024]{1,0:T(8,128)(2,1)S(1)}, u32[]{:S(2)}, u32[]{:S(2)}) collective-permute-start(bf16[352,1024]{1,0:T(8,128)(2,1)} %collective-permute-done.10.refs_2_), channel_id=1, source_target_pairs={{0,3},{1,2},{2,1},{3,0},{4,7},{5,6},{6,5},{7,4},{8,11},{9,10},{10,... | collective-permute-start | bytes 2162696 | tf_op jit(solution)/shard_map/ppermute | solution.py:290
  61.0 56.6 %all-to-all-start = ((bf16[64,16,128]{2,1,0:T(8,128)(2,1)}), bf16[64,16,128]{2,1,0:T(8,128)(2,1)S(1)}, u32[]{:S(2)}, u32[]{:S(2)}) async-start(bf16[64,16,128]{2,1,0:T(8,128)(2,1)} %router.1), calls=%async_computation | async-start | bytes 524288 | tf_op jit(solution)/shard_map/all_to_all | solution.py:317
  94.1 7.4 %collective-permute-start.14 = (bf16[96,1024]{1,0:T(8,128)(2,1)}, bf16[96,1024]{1,0:T(8,128)(2,1)S(1)}, u32[]{:S(2)}, u32[]{:S(2)}) collective-permute-start(bf16[96,1024]{1,0:T(8,128)(2,1)} %get-tuple-element.32.refs_3_), channel_id=1, source_target_pairs={{0,3},{1,2},{2,1},{3,0},{4,7},{5,6},{6,5},{7,4},{8,11},{9,10},{10,... | collective-permute-start | bytes 589832 | tf_op jit(solution)/shard_map/ppermute | solution.py:290
  96.7 18.5 %copy-start.5 = (bf16[16,1024]{1,0:T(8,128)(2,1)}, bf16[16,1024]{1,0:T(8,128)(2,1)S(1)}, u32[]{:S(2)}) copy-start(bf16[16,1024]{1,0:T(8,128)(2,1)S(1)} %divide_convert_fusion.2.refs_1_) | copy-start | bytes 98308
  101.5 2.6 %copy-start.4 = (bf16[96,1024]{1,0:T(8,128)(2,1)}, bf16[96,1024]{1,0:T(8,128)(2,1)S(1)}, u32[]{:S(2)}) copy-start(bf16[96,1024]{1,0:T(8,128)(2,1)S(1)} %collective-permute-done.14.refs_1_) | copy-start | bytes 589828
  101.5 5.4 %collective-permute-start.9 = (bf16[16,1024]{1,0:T(8,128)(2,1)S(1)}, bf16[16,1024]{1,0:T(8,128)(2,1)S(1)}, u32[]{:S(2)}, u32[]{:S(2)}) collective-permute-start(bf16[16,1024]{1,0:T(8,128)(2,1)S(1)} %divide_convert_fusion.2.refs_1_), channel_id=1, source_target_pairs={{0,3},{1,2},{2,1},{3,0},{4,7},{5,6},{6,5},{7,4},{8,11},{9,10},{10,... | collective-permute-start | bytes 98312 | tf_op jit(solution)/shard_map/ppermute | solution.py:290
  106.9 15.6 %collective-permute-start.5 = (bf16[96,1024]{1,0:T(8,128)(2,1)}, bf16[96,1024]{1,0:T(8,128)(2,1)S(1)}, u32[]{:S(2)}, u32[]{:S(2)}) collective-permute-start(bf16[96,1024]{1,0:T(8,128)(2,1)} %copy-done.2), channel_id=1, source_target_pairs={{0,1},{1,0},{2,3},{3,2},{4,5},{5,4},{6,7},{7,6},{8,9},{9,8},{10,11... | collective-permute-start | bytes 589832 | tf_op jit(solution)/shard_map/ppermute | solution.py:290
  106.9 15.6 %collective-permute-start.3 = (bf16[96,1024]{1,0:T(8,128)(2,1)}, bf16[96,1024]{1,0:T(8,128)(2,1)S(1)}, u32[]{:S(2)}, u32[]{:S(2)}) collective-permute-start(bf16[96,1024]{1,0:T(8,128)(2,1)} %collective-permute-done.2.refs_0_), channel_id=1, source_target_pairs={{0,3},{1,2},{2,1},{3,0},{4,7},{5,6},{6,5},{7,4},{8,11},{9,10},{10,... | collective-permute-start | bytes 589832 | tf_op jit(solution)/shard_map/ppermute | solution.py:290
  110.0 5.2 %copy-start.1 = (bf16[48,1024]{1,0:T(8,128)(2,1)}, bf16[48,1024]{1,0:T(8,128)(2,1)S(1)}, u32[]{:S(2)}) copy-start(bf16[48,1024]{1,0:T(8,128)(2,1)S(1)} %get-tuple-element.56.refs_3_) | copy-start | bytes 294916
  110.0 11.2 %collective-permute-start.8 = (bf16[48,1024]{1,0:T(8,128)(2,1)S(1)}, bf16[48,1024]{1,0:T(8,128)(2,1)S(1)}, u32[]{:S(2)}, u32[]{:S(2)}) collective-permute-start(bf16[48,1024]{1,0:T(8,128)(2,1)S(1)} %get-tuple-element.56.refs_3_), channel_id=1, source_target_pairs={{0,1},{1,0},{2,3},{3,2},{4,5},{5,4},{6,7},{7,6},{8,9},{9,8},{10,11... | collective-permute-start | bytes 294920 | tf_op jit(solution)/shard_map/ppermute | solution.py:290
